TPU v7x, 512 devices: a whole 4x8x8 slice. The times are simulated.
512 devices in a mesh: gx: 8 (over z), gy: 16 (over x_lo, y), gz: 4 (over x_hi, core).
Axes of the slice: x: 4 (x_hi: 2, x_lo: 2; x = x_hi * 2 + x_lo), y: 8, z: 8, core: 2. Of those that a mesh axis runs over, the one named last changes fastest.
Arguments:
- colloc: bfloat16 [12288, 4000], P(('gx', 'gy')), may hold values from -6 to 6
- occ_coeffs: bfloat16 [4000, 1024], P(None, 'gz'), may hold values from -0.09375 to 0.09375
- core: bfloat16 [12288, 16, 768], P('gx', 'gy'), may hold values from -3.9041042e-06 to 3.9041042e-06
Outputs:
- coulomb: float32 [96, 4000], P(('gx', 'gz'), 'gy')
- exchange: float32 [96, 4000], P(('gx', 'gz'), 'gy')
All inputs are finite; a program needn't handle non-finite values.
Results may differ from a plain program's by a relative error of at most 0.0089.
Values may be sent and summed in bfloat16 or wider, within the bound.
No kernel may reach another device: no remote copies, remote signals or barrier semaphores. Data moves between devices by JAX's collectives and lax.ppermute only.
A program may use at most 64 MiB of HBM per device.

v0:
```python
import math

import jax
import jax.numpy as jnp
from jax import lax
from jax.sharding import Mesh
from jax.sharding import PartitionSpec as P

W = 96
GY = ("gy_0", "gy_1")
GX_GY = ("gx", "gy_0", "gy_1")


def joined_along(pieces, dim):
    lengths = list(pieces.shape[1:])
    lengths[dim] *= pieces.shape[0]
    return jnp.moveaxis(pieces, 0, dim).reshape(lengths)


def from_everyone(array, axis):
    copies = jnp.broadcast_to(array, (lax.axis_size(axis), *array.shape))
    return lax.all_to_all(copies, axis, split_axis=0, concat_axis=0, tiled=True)


def collect(array, axis, dim):
    return joined_along(from_everyone(array, axis), dim)


def over_copies(array, axis):
    return from_everyone(array, axis).sum(axis=0)


def split_up(array, dim, devices):
    before, after = (array.shape[:dim], array.shape[dim + 1 :])
    return jnp.moveaxis(array.reshape(*before, devices, -1, *after), dim, 0)


def summed_on_arrival(array, axis, dim):
    devices = lax.axis_size(axis)
    pieces = lax.all_to_all(split_up(array, dim, devices), axis, 0, 0, tiled=True)
    return jnp.sum(pieces, axis=0)


def in_one_piece(arrays, axis, dim, along):
    widths = [math.prod(a.shape[along:]) for a in arrays]
    both = jnp.concatenate(
        [a.reshape(*a.shape[:along], w) for a, w in zip(arrays, widths)], axis=along
    )
    filled = lax.all_gather(both, axis, axis=dim, tiled=True)
    pieces = jnp.split(filled, [sum(widths[:k]) for k in range(1, len(widths))], axis=along)
    return tuple(
        (b.reshape(*filled.shape[:along], *a.shape[along:]) for a, b in zip(arrays, pieces))
    )


def sum_at_owner(array, axis, dim):
    pieces = split_up(array, dim, lax.axis_size(axis))
    arrived = lax.all_to_all(pieces, axis, split_axis=0, concat_axis=0, tiled=True)
    return arrived.astype(jnp.float32).sum(axis=0)


def sum_in_two_steps(array, axes, dim):
    far, near = axes
    pieces = split_up(array, dim, lax.axis_size(far))
    nearer = sum_at_owner(pieces, near, dim + 1)
    arrived = lax.all_to_all(
        nearer.astype(jnp.bfloat16), far, split_axis=0, concat_axis=0, tiled=True
    )
    return arrived.astype(jnp.float32).sum(axis=0)


def sent_together(arrays, axis, dim, along):
    widths = [a.shape[along] for a in arrays]
    both = jnp.concatenate(arrays, axis=along)
    filled = sum_in_two_steps(both, axis, dim)
    return tuple(jnp.split(filled, [sum(widths[:k]) for k in range(1, len(widths))], axis=along))


def local(colloc, occ_coeffs, core):
    points, width = colloc.shape
    size_x = lax.axis_size("gx")
    size_y = lax.axis_size(GY)
    size_z = lax.axis_size("gz")
    row_count = core.shape[0]
    flat_cols = core.shape[2]
    col_points = flat_cols // size_x
    per_rows = W // (size_x * size_z)
    occ_vals = jnp.dot(colloc, occ_coeffs, preferred_element_type=jnp.float32).astype(jnp.bfloat16)
    window_vals = colloc[:, :W].reshape(points, size_x, size_z, per_rows)
    window_vals = window_vals.transpose(0, 2, 1, 3).reshape(points, size_z, size_x * per_rows)
    column_vals = collect(occ_vals, "gx", 0)
    square_part = jnp.sum(jnp.square(column_vals.astype(jnp.float32)), axis=1)
    density = over_copies(square_part, "gz").astype(jnp.bfloat16)
    core_flat = core.reshape(row_count, flat_cols)
    potential_rows = jnp.dot(core_flat, density, preferred_element_type=jnp.float32)
    potential = summed_on_arrival(potential_rows, GY, 0)
    occ_piece, win_piece = in_one_piece((occ_vals, window_vals), GY, 0, 1)
    count = occ_piece.shape[0]
    gram = lax.dot_general(
        occ_piece, column_vals, (((1,), (1,)), ((), ())), preferred_element_type=jnp.float32
    )
    mixed = (core_flat.astype(jnp.float32) * gram).astype(jnp.bfloat16)
    mixed = mixed.reshape(count, size_x, col_points)
    totals = jnp.einsum("rap,rgk->agpk", mixed, win_piece, preferred_element_type=jnp.float32)
    weighted = (window_vals.astype(jnp.float32) * potential[:, None, None]).astype(jnp.bfloat16)
    x_cols = colloc.reshape(points, size_y, width // size_y)
    group = lax.axis_index("gz")
    owned = sum_at_owner(
        totals.reshape(size_x * size_z, col_points, size_x * per_rows).astype(jnp.bfloat16),
        ("gx", "gz"),
        0,
    )
    owned = owned[0].astype(jnp.bfloat16)
    mine = lax.dynamic_index_in_dim(weighted, group, 1, keepdims=False)
    coul = jnp.einsum(
        "pbk,pcj->bckj",
        mine.reshape(points, size_x, per_rows),
        x_cols,
        preferred_element_type=jnp.float32,
    )
    exch = jnp.einsum(
        "pbk,pcj->bckj",
        owned.reshape(points, size_x, per_rows),
        x_cols,
        preferred_element_type=jnp.float32,
    )
    coul = coul.reshape(size_x * size_y, per_rows, width // size_y)
    exch = exch.reshape(size_x * size_y, per_rows, width // size_y)
    coul, exch = sent_together(
        (coul.astype(jnp.bfloat16), exch.astype(jnp.bfloat16)), ("gx", ("gy_0", "gy_1")), 0, 1
    )
    coulomb = coul[0]
    exchange = exch[0]
    return (coulomb, exchange)


def solution(mesh):
    split = Mesh(
        mesh.devices.reshape(mesh.shape["gx"], 2, 8, mesh.shape["gz"]), ("gx", "gy_0", "gy_1", "gz")
    )
    return jax.shard_map(
        local,
        mesh=split,
        in_specs=(P(GX_GY, None), P(None, "gz"), P("gx", GY, None)),
        out_specs=(P(("gx", "gz"), GY), P(("gx", "gz"), GY)),
        check_vma=False,
    )
```

profile of v0, /device:TPU:8, one launch (start us, length us, event | category | flops | bytes accessed | tf_op | source)
XLA Modules:
  0.0 150.6 jit_solution(11822203748536144236)
XLA Ops:
  7.2 1.5 %copy-done = bf16[4000,256]{1,0:T(8,128)(2,1)S(1)} copy-done((bf16[4000,256]{1,0:T(8,128)(2,1)S(1)}, bf16[4000,256]{1,0:T(8,128)(2,1)}, u32[]{:S(2)}) %copy-start) | copy-done | bytes 2048024
  8.7 1.6 %convolution_convert_fusion.3 = bf16[96,256]{1,0:T(8,128)(2,1)S(1)} fusion(bf16[96,4000]{1,0:T(8,128)(2,1)} %param.3, bf16[4000,256]{1,0:T(8,128)(2,1)S(1)} %copy-done), kind=kOutput, calls=%fused_computation.8 | convolution fusion | flops 196632576 | bytes 2865152 | tf_op jit(solution)/shard_map/dot_general | solution.py:88
  10.7 0.7 pad_maximum_fusion
  11.4 24.8 %all_to_all.32 = bf16[8,96,256]{2,1,0:T(8,128)(2,1)S(1)} all-to-all(bf16[8,96,256]{2,1,0:T(8,128)(2,1)S(1)} %broadcast_in_dim.9), channel_id=1, replica_groups=mesh['gx'=8,'gy_0'=2,'gy_1'=8,'gz'=4] {'gx'}, dimensions={0} | all-to-all | bytes 786432 | tf_op jit(solution)/shard_map/all_to_all | solution.py:22
  36.2 0.2 multiply_reduce_fusion
  36.5 0.6 broadcast_in_dim.11
  37.1 4.3 %all-to-all-start.1 = ((f32[4,1,768]{2,1,0:T(1,128)}), f32[4,1,768]{2,1,0:T(1,128)S(1)}, u32[]{:S(2)}, u32[]{:S(2)}) async-start(f32[4,1,768]{2,1,0:T(1,128)} %broadcast_in_dim.11), calls=%async_computation.1 | async-start | bytes 24576 | tf_op jit(solution)/shard_map/all_to_all | solution.py:22
  41.4 4.3 %copy.73 = bf16[1536,1,768]{0,2,1:T(8,128)(2,1)} copy(bf16[1536,1,768]{2,0,1:T(8,128)(2,1)} %param.5) | data formatting | bytes 4718592 | tf_op args[2]
  45.7 1.1 all-to-all-done.1
  46.8 3.1 %convolution_bitcast_fusion = f32[16,1,96]{2,1,0:T(1,128)} fusion(bf16[768,1,1]{0,1,2:T(2,128)(2,1)S(1)} %reshape.86, bf16[16,96,768]{2,1,0:T(8,128)(2,1)} %bitcast.63), kind=kOutput, calls=%fused_computation.9 | convolution fusion | flops 2359296 | bytes 2366976 | tf_op jit(solution)/shard_map/dot_general | solution.py:95
  49.8 7.6 %all-to-all-start.2 = ((f32[16,1,96]{2,1,0:T(1,128)}), f32[16,1,96]{2,1,0:T(1,128)S(1)}, u32[]{:S(2)}, u32[]{:S(2)}) async-start(f32[16,1,96]{2,1,0:T(1,128)} %convolution_bitcast_fusion), calls=%async_computation.2 | async-start | bytes 16384 | tf_op jit(solution)/shard_map/all_to_all | solution.py:40
  57.4 29.5 %all-gather.2.cloned.1.call-done = bf16[1536,352]{1,0:T(8,128)(2,1)} async-done(((bf16[96,352]{1,0:T(8,128)(2,1)}), bf16[1536,352]{1,0:T(8,128)(2,1)}) %all-gather.2.cloned.1.call-update) | async-done | bytes 1081360 | tf_op jit(solution)/shard_map/all_gather | solution.py:49
  86.9 1.0 split.16
  88.1 2.7 %fusion = bf16[1536,768]{0,1:T(8,128)(2,1)S(1)} fusion(bf16[768,256]{1,0:T(8,128)(2,1)S(1)} %bitcast.65, bf16[1536,1,768]{0,2,1:T(8,128)(2,1)} %copy.73, bf16[1536,352]{1,0:T(8,128)(2,1)} %all-gather.2.cloned.1.call-done), kind=kOutput, calls=%fused_computation.1 | convolution fusion | flops 607518720 | bytes 5898240 | tf_op jit(solution)/shard_map/dot_general | solution.py:99
  90.8 1.0 fusion.1
  91.8 0.7 copy.74
  92.5 9.8 %all-to-all-start.3 = ((bf16[32,1,96,24]{2,3,1,0:T(8,128)(2,1)}), bf16[32,1,96,24]{2,3,1,0:T(8,128)(2,1)S(1)}, u32[]{:S(2)}, u32[]{:S(2)}) async-start(bf16[32,1,96,24]{2,3,1,0:T(8,128)(2,1)} %bitcast.18), calls=%async_computation.3 | async-start | bytes 393216 | tf_op jit(solution)/shard_map/all_to_all | solution.py:58
  102.4 3.7 %reshape.80 = bf16[96,16,250]{2,1,0:T(8,128)(2,1)S(1)} reshape(bf16[96,4000]{1,0:T(8,128)(2,1)} %param.3) | data formatting | bytes 1536000 | tf_op jit(solution)/shard_map/reshape | solution.py:106
  106.1 0.3 fusion.2
  106.5 7.7 %all-to-all-done.3 = bf16[32,1,96,24]{2,3,1,0:T(8,128)(2,1)S(1)} async-done(((bf16[32,1,96,24]{2,3,1,0:T(8,128)(2,1)}), bf16[32,1,96,24]{2,3,1,0:T(8,128)(2,1)S(1)}, u32[]{:S(2)}, u32[]{:S(2)}) %all-to-all-start.3) | async-done | bytes 147488 | tf_op jit(solution)/shard_map/all_to_all | solution.py:58
  114.2 0.3 fusion.3
  114.7 17.7 %all_to_all.33 = bf16[16,8,1,6,250]{4,1,3,2,0:T(8,128)(2,1)S(1)} all-to-all(bf16[16,8,1,6,250]{4,1,3,2,0:T(8,128)(2,1)S(1)} %copy.77), channel_id=1, replica_groups=mesh['gx'=8,'gy_0'=2,'gy_1'=8,'gz'=4] {'gy_0','gy_1'}, dimensions={0} | all-to-all | bytes 768000 | tf_op jit(solution)/shard_map/all_to_all | solution.py:58
  132.5 10.6 %all_to_all.34 = bf16[8,1,6,250]{3,2,1,0:T(8,128)(2,1)S(1)} all-to-all(bf16[8,1,6,250]{3,2,1,0:T(8,128)(2,1)S(1)} %copy.79), channel_id=1, replica_groups=mesh['gx'=8,'gy_0'=2,'gy_1'=8,'gz'=4] {'gx'}, dimensions={0} | all-to-all | bytes 48000 | tf_op jit(solution)/shard_map/all_to_all | solution.py:66
  143.1 0.6 slice_bitcast_fusion
  (28 shorter events, 1.0 us)
Async XLA Ops:
  7.2 1.6 %copy-start = (bf16[4000,256]{1,0:T(8,128)(2,1)S(1)}, bf16[4000,256]{1,0:T(8,128)(2,1)}, u32[]{:S(2)}) copy-start(bf16[4000,256]{1,0:T(8,128)(2,1)} %param.4) | copy-start | bytes 6144004
  7.2 3.2 %slice-start = ((bf16[96,4000]{1,0:T(8,128)(2,1)}), bf16[96,96]{1,0:T(8,128)(2,1)S(1)}, s32[]{:S(2)}) async-start(bf16[96,4000]{1,0:T(8,128)(2,1)} %param.3), calls=%async_computation.7 | async-start | bytes 49152 | tf_op jit(solution)/shard_map/slice | solution.py:89
  7.2 79.7 %all-gather.2.cloned.1.call-start = ((), (), s32[]{:S(2)}) async-start(), calls=%async_computation.6 | async-start | bytes 1253376 | tf_op jit(solution)/shard_map/all_gather | solution.py:49
  37.1 9.6 %all-to-all-start.1 = ((f32[4,1,768]{2,1,0:T(1,128)}), f32[4,1,768]{2,1,0:T(1,128)S(1)}, u32[]{:S(2)}, u32[]{:S(2)}) async-start(f32[4,1,768]{2,1,0:T(1,128)} %broadcast_in_dim.11), calls=%async_computation.1 | async-start | bytes 24576 | tf_op jit(solution)/shard_map/all_to_all | solution.py:22
  49.8 42.7 %all-to-all-start.2 = ((f32[16,1,96]{2,1,0:T(1,128)}), f32[16,1,96]{2,1,0:T(1,128)S(1)}, u32[]{:S(2)}, u32[]{:S(2)}) async-start(f32[16,1,96]{2,1,0:T(1,128)} %convolution_bitcast_fusion), calls=%async_computation.2 | async-start | bytes 16384 | tf_op jit(solution)/shard_map/all_to_all | solution.py:40
  92.5 21.6 %all-to-all-start.3 = ((bf16[32,1,96,24]{2,3,1,0:T(8,128)(2,1)}), bf16[32,1,96,24]{2,3,1,0:T(8,128)(2,1)S(1)}, u32[]{:S(2)}, u32[]{:S(2)}) async-start(bf16[32,1,96,24]{2,3,1,0:T(8,128)(2,1)} %bitcast.18), calls=%async_computation.3 | async-start | bytes 393216 | tf_op jit(solution)/shard_map/all_to_all | solution.py:58
Sparse Core Ops, SparseCore 0:
  11.5 75.3 all-gather.1
where the time goes:
time: 151 us
  blocking collectives  53.1 us (35%)
  waiting for transfers between devices  38.2 us (25%)
  starting transfers between devices  21.7 us (14%)
  between operations  14.2 us (9%)
  local copies, waits for them, and re-layouts  13 us (9%)
  matrix products  9.04 us (6%)
    all_gather x1, waiting for transfers between devices, in_one_piece(): filled = lax.all_gather(both, axis, axis=dim, tiled=True)  29.5 us
    all_to_all x1, blocking collectives, from_everyone(): return lax.all_to_all(copies, axis, split_axis=0, concat_axis=0, tiled=True)  24.8 us
    all_to_all x1, blocking collectives, sum_at_owner(): lax.all_to_all(pieces, axis, split_axis=0, concat_axis=0, tiled=True)  17.7 us
    all_to_all x1, blocking collectives, sum_in_two_steps(): lax.all_to_all(nearer.astype(jnp.bfloat16), far, split_axis=0, concat_axi...  10.6 us
    all_to_all x1, starting transfers between devices, sum_at_owner(): lax.all_to_all(pieces, axis, split_axis=0, concat_axis=0, tiled=True)  9.8 us
    all_to_all x1, waiting for transfers between devices, sum_at_owner(): lax.all_to_all(pieces, axis, split_axis=0, concat_axis=0, tiled=True)  7.71 us
    all_to_all x1, starting transfers between devices, summed_on_arrival(): lax.all_to_all(split_up(array, dim, devices), axis, 0, 0, tiled=True)  7.6 us
    unnamed x3, local copies, waits for them, and re-layouts  5.8 us
  transfers between devices with their start and end apart: 4, of which 3 were waited for; matrix products, arithmetic and copies ran while one was open for 12% of the time, Pallas kernels for 0%

commit v1 on v0

v1 whole, which is shorter than its diff:
```python
import jax
import jax.numpy as jnp
from jax import lax
from jax.sharding import Mesh
from jax.sharding import PartitionSpec as P

W = 96
GY = ("gy_0", "gy_1")
GX_GY = ("gx", "gy_0", "gy_1")


def exchange_pieces(pieces, axis):
    return lax.all_to_all(pieces, axis, split_axis=0, concat_axis=0, tiled=True)


def from_everyone(array, axis):
    copies = jnp.broadcast_to(array, (lax.axis_size(axis), *array.shape))
    return exchange_pieces(copies, axis)


def three_pieces(value):
    high = value.astype(jnp.bfloat16)
    rest = value - high.astype(jnp.float32)
    middle = rest.astype(jnp.bfloat16)
    low = (rest - middle.astype(jnp.float32)).astype(jnp.bfloat16)
    return jnp.stack([high, middle, low])


def local(colloc, occ_coeffs, core):
    points, width = colloc.shape
    size_x = lax.axis_size("gx")
    size_y = lax.axis_size(GY)
    size_z = lax.axis_size("gz")
    row_count = core.shape[0]
    flat_cols = core.shape[2]
    col_points = flat_cols // size_x
    per_rows = W // (size_x * size_z)
    own = size_x * per_rows
    core_flat = core.reshape(row_count, flat_cols)

    occ_vals = jnp.dot(colloc, occ_coeffs, preferred_element_type=jnp.float32).astype(jnp.bfloat16)
    window = colloc[:, :W].reshape(points, size_x, size_z, per_rows)
    window = window.transpose(0, 2, 1, 3).reshape(points, W)

    row_vals = from_everyone(jnp.concatenate([occ_vals, window], axis=1), GY)
    col_vals = from_everyone(occ_vals, "gx").reshape(flat_cols, -1)
    row_vals = row_vals.reshape(row_count, -1)
    row_occ = row_vals[:, : occ_vals.shape[1]]
    row_win = row_vals[:, occ_vals.shape[1] :]

    density = jnp.sum(jnp.square(col_vals.astype(jnp.float32)), axis=1).astype(jnp.bfloat16)
    potential_rows = jnp.dot(core_flat, density, preferred_element_type=jnp.float32)
    potential = exchange_pieces(potential_rows.reshape(size_y, points), GY).sum(axis=0)

    gram = lax.dot_general(
        row_occ, col_vals, (((1,), (1,)), ((), ())), preferred_element_type=jnp.float32
    )
    mixed = (core_flat.astype(jnp.float32) * gram).astype(jnp.bfloat16)
    totals = lax.dot_general(
        row_win, mixed, (((0,), (0,)), ((), ())), preferred_element_type=jnp.float32
    ).astype(jnp.bfloat16)
    totals = totals.reshape(size_z, own, size_x, col_points).transpose(2, 0, 1, 3)

    mine = lax.axis_index("gx") == jnp.arange(size_x)
    carried = jnp.where(mine[:, None, None, None], three_pieces(potential)[None, None], 0)
    carried = jnp.broadcast_to(carried, (size_x, size_z, 3, col_points)).astype(jnp.bfloat16)
    sent = jnp.concatenate([totals, carried], axis=2)
    sent = sent.reshape(size_x * size_z, own + 3, col_points)
    owned = exchange_pieces(sent, ("gx", "gz")).astype(jnp.float32).sum(axis=0)

    total_own = owned[:own]
    potential_own = owned[own:].sum(axis=0)
    window_own = lax.dynamic_index_in_dim(
        window.reshape(points, size_z, own), lax.axis_index("gz"), 1, keepdims=False
    )
    weighted = window_own.T.astype(jnp.float32) * potential_own[None, :]
    left = jnp.stack(
        [weighted.reshape(size_x, per_rows, points), total_own.reshape(size_x, per_rows, points)],
        axis=1,
    )
    left = left.reshape(2 * own, points).astype(jnp.bfloat16)
    x_cols = colloc.reshape(points, size_y, width // size_y)
    both = jnp.einsum("mp,pcj->cmj", left, x_cols, preferred_element_type=jnp.float32)
    both = exchange_pieces(both.astype(jnp.bfloat16), GY).astype(jnp.float32).sum(axis=0)
    both = both.astype(jnp.bfloat16).reshape(size_x, 2 * per_rows, width // size_y)
    both = exchange_pieces(both, "gx").astype(jnp.float32).sum(axis=0)
    return (both[:per_rows], both[per_rows:])


def solution(mesh):
    split = Mesh(
        mesh.devices.reshape(mesh.shape["gx"], 2, 8, mesh.shape["gz"]), ("gx", "gy_0", "gy_1", "gz")
    )
    return jax.shard_map(
        local,
        mesh=split,
        in_specs=(P(GX_GY, None), P(None, "gz"), P("gx", GY, None)),
        out_specs=(P(("gx", "gz"), GY), P(("gx", "gz"), GY)),
        check_vma=False,
    )
```

time: 151 us -> 137 us (0.907)
  the two profiles are of different devices: /device:TPU:8 before, /device:TPU:10 now
where the time goes in v1:
time: 137 us; the launch traced here: 136 us
  waiting for transfers between devices  56.9 us (42%)
  blocking collectives  29.8 us (22%)
  starting transfers between devices  29 us (21%)
  matrix products  9.68 us (7%)
  local copies, waits for them, and re-layouts  9.21 us (7%)
    all_to_all x4, waiting for transfers between devices, exchange_pieces(): return lax.all_to_all(pieces, axis, split_axis=0, concat_axis=0, tiled=True)  56.9 us
    all_to_all x2, blocking collectives, exchange_pieces(): return lax.all_to_all(pieces, axis, split_axis=0, concat_axis=0, tiled=True)  29.8 us
    all_to_all x4, starting transfers between devices, exchange_pieces(): return lax.all_to_all(pieces, axis, split_axis=0, concat_axis=0, tiled=True)  29 us
    dot_general x1, matrix products, local(): lax.dot_general(row_win, mixed, (((0,), (0,)), ((), ())), preferred_eleme...  3.48 us
    reshape x1, local copies, waits for them, and re-layouts, local(): x_cols = colloc.reshape(points, size_y, width // size_y)  3.46 us
    dot_general x1, matrix products, local(): jnp.dot(core_flat, density, preferred_element_type=jnp.float32)  3.09 us
  transfers between devices with their start and end apart: 4, of which 4 were waited for; matrix products, arithmetic and copies ran while one was open for 3% of the time, Pallas kernels for 0%

profile of v1, /device:TPU:10, one launch (start us, length us, event | category | flops | bytes accessed | tf_op | source)
XLA Modules:
  0.0 136.2 jit_solution(2648560914527585453)
XLA Ops:
  0.7 1.6 %copy-done = bf16[4000,256]{1,0:T(8,128)(2,1)S(1)} copy-done((bf16[4000,256]{1,0:T(8,128)(2,1)S(1)}, bf16[4000,256]{1,0:T(8,128)(2,1)}, u32[]{:S(2)}) %copy-start) | copy-done | bytes 2048024
  2.2 1.6 %convolution_convert_fusion.1 = bf16[96,256]{1,0:T(8,128)(2,1)S(1)} fusion(bf16[96,4000]{1,0:T(8,128)(2,1)} %param.3, bf16[4000,256]{1,0:T(8,128)(2,1)S(1)} %copy-done), kind=kOutput, calls=%fused_computation.6 | convolution fusion | flops 196632576 | bytes 2865152 | tf_op jit(solution)/shard_map/dot_general | solution.py:41
  3.8 0.8 broadcast_in_dim.35
  4.6 10.3 %all-to-all-start.1 = ((bf16[8,96,256]{2,1,0:T(8,128)(2,1)}), bf16[8,96,256]{2,1,0:T(8,128)(2,1)S(1)}, u32[]{:S(2)}, u32[]{:S(2)}) async-start(bf16[8,96,256]{2,1,0:T(8,128)(2,1)} %broadcast_in_dim.35), calls=%async_computation.1 | async-start | bytes 786432 | tf_op jit(solution)/shard_map/all_to_all | solution.py:13
  15.2 14.4 %all-to-all-done.1 = bf16[8,96,256]{2,1,0:T(8,128)(2,1)S(1)} async-done(((bf16[8,96,256]{2,1,0:T(8,128)(2,1)}), bf16[8,96,256]{2,1,0:T(8,128)(2,1)S(1)}, u32[]{:S(2)}, u32[]{:S(2)}) %all-to-all-start.1) | async-done | bytes 393248 | tf_op jit(solution)/shard_map/all_to_all | solution.py:13
  29.6 0.2 multiply_reduce_fusion
  29.9 3.1 %convolution_bitcast_fusion = f32[16,1,96]{2,1,0:T(1,128)} fusion(bf16[768,1,1]{0,1,2:T(2,128)(2,1)S(1)} %reshape.116, bf16[16,96,768]{2,1,0:T(8,128)(2,1)} %bitcast.48), kind=kOutput, calls=%fused_computation.7 | convolution fusion | flops 2359296 | bytes 2366976 | tf_op jit(solution)/shard_map/dot_general | solution.py:52
  33.0 8.5 %all-to-all-start.2 = ((f32[16,1,96]{2,1,0:T(1,128)}), f32[16,1,96]{2,1,0:T(1,128)S(1)}, u32[]{:S(2)}, u32[]{:S(2)}) async-start(f32[16,1,96]{2,1,0:T(1,128)} %convolution_bitcast_fusion), calls=%async_computation.2 | async-start | bytes 16384 | tf_op jit(solution)/shard_map/all_to_all | solution.py:13
  41.5 6.2 %all-to-all-done.2 = f32[16,1,96]{2,1,0:T(1,128)S(1)} async-done(((f32[16,1,96]{2,1,0:T(1,128)}), f32[16,1,96]{2,1,0:T(1,128)S(1)}, u32[]{:S(2)}, u32[]{:S(2)}) %all-to-all-start.2) | async-done | bytes 6176 | tf_op jit(solution)/shard_map/all_to_all | solution.py:13
  47.7 1.2 broadcast_in_dim.34
  48.8 6.3 %all-to-all-start = ((bf16[16,96,352]{2,1,0:T(8,128)(2,1)}), bf16[16,96,352]{2,1,0:T(8,128)(2,1)}, u32[]{:S(2)}, u32[]{:S(2)}) async-start(bf16[16,96,352]{2,1,0:T(8,128)(2,1)} %broadcast_in_dim.34), calls=%async_computation | async-start | bytes 2359296 | tf_op jit(solution)/shard_map/all_to_all | solution.py:13
  55.3 26.7 %all-to-all-done = bf16[16,96,352]{2,1,0:T(8,128)(2,1)} async-done(((bf16[16,96,352]{2,1,0:T(8,128)(2,1)}), bf16[16,96,352]{2,1,0:T(8,128)(2,1)}, u32[]{:S(2)}, u32[]{:S(2)}) %all-to-all-start) | async-done | bytes 1081376 | tf_op jit(solution)/shard_map/all_to_all | solution.py:13
  82.0 3.5 %fusion.3 = bf16[96,768]{1,0:T(8,128)(2,1)S(1)} fusion(bf16[768,256]{1,0:T(8,128)(2,1)S(1)} %bitcast.49, bf16[1536,1,768]{2,0,1:T(8,128)(2,1)} %param.5, bf16[1536,352]{1,0:T(8,128)(2,1)} %bitcast.3), kind=kOutput, calls=%fused_computation.5 | convolution fusion | flops 834084864 | bytes 3981312 | tf_op jit(solution)/shard_map/dot_general | solution.py:59
  85.5 0.2 reshape.109
  85.8 0.2 copy.35
  85.9 0.2 pad_maximum_fusion
  86.1 0.8 copy.28
  86.9 3.9 %all-to-all-start.3 = ((bf16[32,27,96]{2,1,0:T(8,128)(2,1)}), bf16[32,27,96]{2,1,0:T(8,128)(2,1)S(1)}, u32[]{:S(2)}, u32[]{:S(2)}) async-start(bf16[32,27,96]{2,1,0:T(8,128)(2,1)} %copy.28), calls=%async_computation.3 | async-start | bytes 524288 | tf_op jit(solution)/shard_map/all_to_all | solution.py:13
  90.9 3.5 %reshape.112 = bf16[96,16,250]{2,1,0:T(8,128)(2,1)} reshape(bf16[96,4000]{1,0:T(8,128)(2,1)S(1)} %copy-done.1) | data formatting | bytes 1536000 | tf_op jit(solution)/shard_map/reshape | solution.py:82
  94.4 9.6 %all-to-all-done.3 = bf16[32,27,96]{2,1,0:T(8,128)(2,1)S(1)} async-done(((bf16[32,27,96]{2,1,0:T(8,128)(2,1)}), bf16[32,27,96]{2,1,0:T(8,128)(2,1)S(1)}, u32[]{:S(2)}, u32[]{:S(2)}) %all-to-all-start.3) | async-done | bytes 165920 | tf_op jit(solution)/shard_map/all_to_all | solution.py:13
  104.2 1.5 %fusion.2 = bf16[16,48,250]{2,1,0:T(8,128)(2,1)S(1)} fusion(bf16[48,96,1]{1,0,2:T(8,128)(2,1)S(1)} %reshape.118, bf16[96,16,250]{2,1,0:T(8,128)(2,1)} %reshape.112), kind=kOutput, calls=%fused_computation.4 | convolution fusion | flops 37056000 | bytes 1161216 | tf_op jit(solution)/shard_map/mp,pcj->cmj/dot_general | solution.py:83
  105.7 18.5 %all_to_all.31 = bf16[16,48,250]{2,1,0:T(8,128)(2,1)S(1)} all-to-all(bf16[16,48,250]{2,1,0:T(8,128)(2,1)S(1)} %fusion.2), channel_id=1, replica_groups=mesh['gx'=8,'gy_0'=2,'gy_1'=8,'gz'=4] {'gy_0','gy_1'}, dimensions={0} | all-to-all | bytes 768000 | tf_op jit(solution)/shard_map/all_to_all | solution.py:13
  124.3 11.2 %all_to_all.32 = bf16[8,6,250]{2,1,0:T(8,128)(2,1)S(1)} all-to-all(bf16[8,6,250]{2,1,0:T(8,128)(2,1)S(1)} %reshape.113), channel_id=1, replica_groups=mesh['gx'=8,'gy_0'=2,'gy_1'=8,'gz'=4] {'gx'}, dimensions={0} | all-to-all | bytes 48000 | tf_op jit(solution)/shard_map/all_to_all | solution.py:13
  135.6 0.6 fusion.10
  (33 shorter events, 0.8 us)
Async XLA Ops:
  0.6 1.6 %copy-start = (bf16[4000,256]{1,0:T(8,128)(2,1)S(1)}, bf16[4000,256]{1,0:T(8,128)(2,1)}, u32[]{:S(2)}) copy-start(bf16[4000,256]{1,0:T(8,128)(2,1)} %param.4) | copy-start | bytes 6144004
  0.6 14.2 %slice-start = ((bf16[96,4000]{1,0:T(8,128)(2,1)}), bf16[96,96]{1,0:T(8,128)(2,1)S(1)}, s32[]{:S(2)}) async-start(bf16[96,4000]{1,0:T(8,128)(2,1)} %param.3), calls=%async_computation.6 | async-start | bytes 49152 | tf_op jit(solution)/shard_map/slice | solution.py:42
  4.6 25.0 %all-to-all-start.1 = ((bf16[8,96,256]{2,1,0:T(8,128)(2,1)}), bf16[8,96,256]{2,1,0:T(8,128)(2,1)S(1)}, u32[]{:S(2)}, u32[]{:S(2)}) async-start(bf16[8,96,256]{2,1,0:T(8,128)(2,1)} %broadcast_in_dim.35), calls=%async_computation.1 | async-start | bytes 786432 | tf_op jit(solution)/shard_map/all_to_all | solution.py:13
  33.0 14.7 %all-to-all-start.2 = ((f32[16,1,96]{2,1,0:T(1,128)}), f32[16,1,96]{2,1,0:T(1,128)S(1)}, u32[]{:S(2)}, u32[]{:S(2)}) async-start(f32[16,1,96]{2,1,0:T(1,128)} %convolution_bitcast_fusion), calls=%async_computation.2 | async-start | bytes 16384 | tf_op jit(solution)/shard_map/all_to_all | solution.py:13
  48.8 33.2 %all-to-all-start = ((bf16[16,96,352]{2,1,0:T(8,128)(2,1)}), bf16[16,96,352]{2,1,0:T(8,128)(2,1)}, u32[]{:S(2)}, u32[]{:S(2)}) async-start(bf16[16,96,352]{2,1,0:T(8,128)(2,1)} %broadcast_in_dim.34), calls=%async_computation | async-start | bytes 2359296 | tf_op jit(solution)/shard_map/all_to_all | solution.py:13
  85.5 5.4 %copy-start.1 = (bf16[96,4000]{1,0:T(8,128)(2,1)S(1)}, bf16[96,4000]{1,0:T(8,128)(2,1)}, u32[]{:S(2)}) copy-start(bf16[96,4000]{1,0:T(8,128)(2,1)} %param.3) | copy-start | bytes 2304004
  86.9 17.0 %all-to-all-start.3 = ((bf16[32,27,96]{2,1,0:T(8,128)(2,1)}), bf16[32,27,96]{2,1,0:T(8,128)(2,1)S(1)}, u32[]{:S(2)}, u32[]{:S(2)}) async-start(bf16[32,27,96]{2,1,0:T(8,128)(2,1)} %copy.28), calls=%async_computation.3 | async-start | bytes 524288 | tf_op jit(solution)/shard_map/all_to_all | solution.py:13

commit v2 on v1

v2 whole, which is shorter than its diff:
```python
import functools

import jax
import jax.numpy as jnp
from jax import lax
from jax.experimental import pallas as pl
from jax.experimental.pallas import tpu as pltpu
from jax.sharding import Mesh
from jax.sharding import PartitionSpec as P

W = 96
LANES = 128
GRANT = 24 * 1024 * 1024
GY = ("gy_0", "gy_1")
GX_GY = ("gx", "gy_0", "gy_1")
BF16 = jnp.bfloat16
F32 = jnp.float32
IN_VMEM = pl.BlockSpec(memory_space=pltpu.VMEM)
IN_HBM = pl.BlockSpec(memory_space=pl.ANY)
IN_SMEM = pl.BlockSpec(memory_space=pltpu.SMEM)


def exchange_pieces(pieces, axis):
    return lax.all_to_all(pieces, axis, split_axis=0, concat_axis=0, tiled=True)


def one_hot(shape, target):
    rows = lax.broadcasted_iota(jnp.int32, shape, 0)
    cols = lax.broadcasted_iota(jnp.int32, shape, 1)
    return jnp.where(cols == target(rows), 1.0, 0.0).astype(BF16)


def times(left, right, left_dim=1, right_dim=0):
    dims = (((left_dim,), (right_dim,)), ((), ()))
    return lax.dot_general(left, right, dims, preferred_element_type=F32)


def three_pieces(value):
    high = value.astype(BF16).astype(F32)
    middle = (value - high).astype(BF16).astype(F32)
    return high, middle, value - high - middle


def occupied(sizes, chunk, _, colloc_hbm, coeffs_hbm, copies, block, colloc, coeffs, sems):
    size_x, size_z, per_rows = sizes
    width, group = coeffs.shape
    starts = range(0, width, chunk)
    copies_in = []
    for k, at in enumerate(starts):
        part = pl.ds(at, min(chunk, width - at))
        copies_in.append(
            (
                pltpu.make_async_copy(colloc_hbm.at[:, part], colloc.at[:, part], sems.at[0, k]),
                pltpu.make_async_copy(coeffs_hbm.at[part, :], coeffs.at[part, :], sems.at[1, k]),
            )
        )
    for first, second in copies_in:
        first.start()
        second.start()
    acc = jnp.zeros((colloc.shape[0], group), F32)
    for (first, second), at in zip(copies_in, starts):
        first.wait()
        second.wait()
        part = pl.ds(at, min(chunk, width - at))
        acc += times(colloc[:, part], coeffs[part, :])
    occ = acc.astype(BF16)
    for a in range(size_x):
        copies[a] = occ
    own = size_x * per_rows

    def source(col):
        return ((col % own) // per_rows) * (size_z * per_rows) + (col // own) * per_rows + col % per_rows

    pick = one_hot((LANES, LANES), lambda rows: jnp.where(rows < W, source(rows), -1))
    window = times(colloc[:, :LANES], pick, 1, 1)
    block[:, :group] = occ
    block[:, group:] = window.astype(BF16)


def potential_rows(cols, block, core, copies):
    size_x, points, group = cols.shape
    size_y = copies.shape[0]
    vals = cols[...].reshape(size_x * points, group).astype(F32)
    density = jnp.sum(vals * vals, axis=1, keepdims=True).astype(BF16)
    density = jnp.broadcast_to(density, (size_x * points, LANES))
    lane = lax.broadcasted_iota(jnp.int32, (points, LANES), 1)
    occ = block[:, :group]
    window = block[:, group:].astype(F32)
    for c in range(size_y):
        share = times(core[pl.ds(c * points, points), :], density)
        high, middle, low = three_pieces(share)
        tail = jnp.where(lane == W, high, window)
        tail = jnp.where(lane == W + 1, middle, tail)
        tail = jnp.where(lane == W + 2, low, tail)
        copies[c, :, :group] = occ
        copies[c, :, group:] = tail.astype(BF16)


def partial_totals(sizes, per_step, place, rows, cols, core, sent):
    size_x, size_z, per_rows = sizes
    size_y, points, _ = rows.shape
    group = cols.shape[2]
    own = size_x * per_rows
    right = cols[...].reshape(size_x * points, group)
    totals = jnp.zeros((LANES, size_x * points), F32)
    tails = jnp.zeros((points, LANES), F32)
    for c in range(0, size_y, per_step):
        height = per_step * points
        left = rows[pl.ds(c, per_step), :, :group].reshape(height, group)
        tail = rows[pl.ds(c, per_step), :, group:].reshape(height, LANES)
        gram = times(left, right, 1, 1)
        mixed = (core[pl.ds(c * points, height), :].astype(F32) * gram).astype(BF16)
        totals += times(tail, mixed, 0, 0)
        for step in range(per_step):
            tails += tail[step * points : (step + 1) * points].astype(F32)
    lane = lax.broadcasted_iota(jnp.int32, (points, LANES), 1)
    share = jnp.sum(jnp.where(lane < W, 0.0, tails), axis=1, keepdims=True)
    high, middle, low = three_pieces(share)
    pieces = jnp.where(lane == 0, high, jnp.where(lane == 1, middle, jnp.where(lane == 2, low, 0.0)))
    square = one_hot((points, points), lambda rows: rows)
    pieces = times(pieces.astype(BF16), square, 0, 0)[: sent.shape[1] - own]
    for a in range(size_x):
        carried = jnp.where(place[0] == a, pieces, 0.0).astype(BF16)
        for g in range(size_z):
            part = totals[g * own : (g + 1) * own, a * points : (a + 1) * points]
            sent[a * size_z + g, :own] = part.astype(BF16)
            sent[a * size_z + g, own:] = carried


def final_shares(sizes, place, arrived, block, colloc, shares, rows):
    size_x, size_z, per_rows = sizes
    size_y, height, part = shares.shape
    own = size_x * per_rows
    total = jnp.sum(arrived[...].astype(F32), axis=0)
    potential = jnp.sum(total[own:], axis=0, keepdims=True)
    window = block[:, block.shape[1] - LANES :]
    pick = one_hot((own, LANES), lambda row: row + place[1] * own)
    weighted = (times(pick, window, 1, 1) * potential).astype(BF16)

    def spread(which):
        def target(row):
            inside = row % (2 * per_rows)
            found = (row // (2 * per_rows)) * per_rows + inside % per_rows
            return jnp.where(inside // per_rows == which, found, -1)

        return one_hot((height, own), target)

    left = times(spread(0), weighted) + times(spread(1), total[:own].astype(BF16))
    rows[:, : colloc.shape[1]] = times(left.astype(BF16), colloc[...])
    for c in range(size_y):
        start = (c * part) // LANES * LANES
        span = -(-(c * part + part - start) // LANES) * LANES
        found = rows[:, pl.ds(start, span)]
        shift = c * part - start
        if shift:
            found = pltpu.roll(found, span - shift, 1)
        shares[c] = found[:, :part].astype(BF16)


def local(colloc, occ_coeffs, core):
    points, width = colloc.shape
    group = occ_coeffs.shape[1]
    size_x = lax.axis_size("gx")
    size_y = lax.axis_size(GY)
    size_z = lax.axis_size("gz")
    row_count = core.shape[0]
    flat_cols = core.shape[2]
    per_rows = W // (size_x * size_z)
    own = size_x * per_rows
    part = width // size_y
    sizes = (size_x, size_z, per_rows)
    core_flat = core.reshape(row_count, flat_cols)
    place = jnp.stack([lax.axis_index("gx"), lax.axis_index("gz")]).astype(jnp.int32)
    chunk = 8 * LANES
    steps = -(-width // chunk)

    copies, block = pl.pallas_call(
        functools.partial(occupied, sizes, chunk),
        in_specs=[IN_SMEM, IN_HBM, IN_HBM],
        out_specs=[IN_VMEM, IN_VMEM],
        out_shape=[
            jax.ShapeDtypeStruct((size_x, points, group), BF16),
            jax.ShapeDtypeStruct((points, group + LANES), BF16),
        ],
        scratch_shapes=[
            pltpu.VMEM((points, width), BF16),
            pltpu.VMEM((width, group), BF16),
            pltpu.SemaphoreType.DMA((2, steps)),
        ],
        compiler_params=pltpu.CompilerParams(vmem_limit_bytes=GRANT),
        name="occupied",
    )(place, colloc, occ_coeffs)
    cols = exchange_pieces(copies, "gx")

    row_copies = pl.pallas_call(
        potential_rows,
        in_specs=[IN_VMEM, IN_VMEM, IN_VMEM],
        out_specs=IN_VMEM,
        out_shape=jax.ShapeDtypeStruct((size_y, points, group + LANES), BF16),
        compiler_params=pltpu.CompilerParams(vmem_limit_bytes=GRANT),
        name="potential_rows",
    )(cols, block, core_flat)
    rows = exchange_pieces(row_copies, GY)

    sent = pl.pallas_call(
        functools.partial(partial_totals, sizes, 4),
        in_specs=[IN_SMEM, IN_VMEM, IN_VMEM, IN_VMEM],
        out_specs=IN_VMEM,
        out_shape=jax.ShapeDtypeStruct((size_x * size_z, own + 8, points), BF16),
        compiler_params=pltpu.CompilerParams(vmem_limit_bytes=GRANT),
        name="partial_totals",
    )(place, rows, cols, core_flat)
    arrived = exchange_pieces(sent, ("gx", "gz"))

    shares = pl.pallas_call(
        functools.partial(final_shares, sizes),
        in_specs=[IN_SMEM, IN_VMEM, IN_VMEM, IN_VMEM],
        out_specs=IN_VMEM,
        out_shape=jax.ShapeDtypeStruct((size_y, 2 * own, part), BF16),
        scratch_shapes=[pltpu.VMEM((2 * own, -(-width // LANES) * LANES), F32)],
        compiler_params=pltpu.CompilerParams(vmem_limit_bytes=GRANT),
        name="final_shares",
    )(place, arrived, block, colloc)
    both = exchange_pieces(shares, GY).astype(F32).sum(axis=0)
    both = both.astype(BF16).reshape(size_x, 2 * per_rows, part)
    both = exchange_pieces(both, "gx").astype(F32).sum(axis=0)
    return (both[:per_rows], both[per_rows:])


def solution(mesh):
    split = Mesh(
        mesh.devices.reshape(mesh.shape["gx"], 2, 8, mesh.shape["gz"]), ("gx", "gy_0", "gy_1", "gz")
    )
    return jax.shard_map(
        local,
        mesh=split,
        in_specs=(P(GX_GY, None), P(None, "gz"), P("gx", GY, None)),
        out_specs=(P(("gx", "gz"), GY), P(("gx", "gz"), GY)),
        check_vma=False,
    )
```

time: 137 us -> 119 us (0.87)
  blocking collectives: 29.8 us -> 108 us
  waiting for transfers between devices: 56.9 us -> 0 us
  starting transfers between devices: 29 us -> 0 us
  matrix products: 9.68 us -> 0 us
  Pallas kernels: 0 us -> 6.28 us
  local copies, waits for them, and re-layouts: 9.21 us -> 3.48 us
    all_to_all x2 -> x5, blocking collectives: 29.8 us -> 108 us  [exchange_pieces(): return lax.all_to_all(pieces, axis, split_axis=0, concat_axis=0, tiled=True)]
    all_to_all x4 -> x0, waiting for transfers between devices: 56.9 us -> none  [exchange_pieces(): return lax.all_to_all(pieces, axis, split_axis=0, concat_axis=0, tiled=True)]
    all_to_all x4 -> x0, starting transfers between devices: 29 us -> none  [exchange_pieces(): return lax.all_to_all(pieces, axis, split_axis=0, concat_axis=0, tiled=True)]
    dot_general x4 -> x0, matrix products: 9.68 us -> none  [the longest x1 3.48 us: local(): lax.dot_general(row_win, mixed, (((0,), (0,)), ((), ())), preferred_eleme...]
    pallas_call x0 -> x4, Pallas kernels: none -> 6.28 us  [the longest x1 2.19 us: local(): pl.pallas_call(functools.partial(partial_totals, sizes, 4), in_specs=[IN_...]
    reshape x8 -> x1, local copies, waits for them, and re-layouts: 4.84 us -> 0.02 us  [local(): both = both.astype(BF16).reshape(size_x, 2 * per_rows, part)]
    broadcast_in_dim x3 -> x0, local copies, waits for them, and re-layouts: 1.92 us -> none  [the longest x2 1.92 us: from_everyone(): copies = jnp.broadcast_to(array, (lax.axis_size(axis), *array.shape))]
    unnamed x4 -> x8, local copies, waits for them, and re-layouts: 1.57 us -> 2.86 us
  transfers between devices with their start and end apart: 4 -> 0, of which waited for: 4 -> 0; matrix products, arithmetic and copies ran while one was open for 3% -> 0% of each run, Pallas kernels for 0% -> 0%
where the time goes in v2:
time: 119 us
  blocking collectives  108 us (91%)
  Pallas kernels  6.28 us (5%)
  local copies, waits for them, and re-layouts  3.48 us (3%)
    all_to_all x5, blocking collectives, exchange_pieces(): return lax.all_to_all(pieces, axis, split_axis=0, concat_axis=0, tiled=True)  108 us
    unnamed x8, local copies, waits for them, and re-layouts  2.86 us

profile of v2, /device:TPU:10, one launch (start us, length us, event | category | flops | bytes accessed | tf_op | source)
XLA Modules:
  0.0 118.7 jit_solution(8413838860015477192)
XLA Ops:
  0.6 0.0 copy-start
  0.6 0.1 pad_add_fusion._.place
  0.7 0.0 copy-start.1
  0.7 1.3 %copy-done.1 = bf16[96,4000]{1,0:T(8,128)(2,1)S(1)} copy-done((bf16[96,4000]{1,0:T(8,128)(2,1)S(1)}, bf16[96,4000]{1,0:T(8,128)(2,1)}, u32[]{:S(2)}) %copy-start.1) | copy-done | bytes 768024
  2.0 0.0 copy-start.3
  2.0 1.6 %copy-done.3 = bf16[4000,256]{1,0:T(8,128)(2,1)S(1)} copy-done((bf16[4000,256]{1,0:T(8,128)(2,1)S(1)}, bf16[4000,256]{1,0:T(8,128)(2,1)}, u32[]{:S(2)}) %copy-start.3) | copy-done | bytes 2048024
  3.6 2.0 %occupied.1 = (bf16[8,96,256]{2,1,0:T(8,128)(2,1)S(1)}, bf16[96,384]{1,0:T(8,128)(2,1)S(1)}) custom-call(s32[2]{0:T(128)S(1)} %pad_add_fusion._.place, bf16[96,4000]{1,0:T(8,128)(2,1)S(1)} %copy-done.1, bf16[4000,256]{1,0:T(8,128)(2,1)S(1)} %copy-done.3), custom_call_target="tpu_custom_call" | custom-call | tf_op jit(solution)/shard_map/occupied/pallas_call | solution.py:177
  5.6 24.8 %all_to_all.25.cols = bf16[8,96,256]{2,1,0:T(8,128)(2,1)S(1)} all-to-all(bf16[8,96,256]{2,1,0:T(8,128)(2,1)S(1)} %get-tuple-element.4), channel_id=1, replica_groups=mesh['gx'=8,'gy_0'=2,'gy_1'=8,'gz'=4] {'gx'}, dimensions={0} | all-to-all | bytes 786432 | tf_op jit(solution)/shard_map/all_to_all | solution.py:24
  30.4 0.0 copy-done
  30.4 0.9 potential_rows.1
  31.3 36.7 %all_to_all.26.rows = bf16[16,96,384]{2,1,0:T(8,128)(2,1)S(1)} all-to-all(bf16[16,96,384]{2,1,0:T(8,128)(2,1)S(1)} %potential_rows.1), channel_id=1, replica_groups=mesh['gx'=8,'gy_0'=2,'gy_1'=8,'gz'=4] {'gy_0','gy_1'}, dimensions={0} | all-to-all | bytes 2359296 | tf_op jit(solution)/shard_map/all_to_all | solution.py:24
  68.0 0.0 copy-start.2
  68.0 2.2 %partial_totals.1 = bf16[32,32,96]{2,1,0:T(8,128)(2,1)S(1)} custom-call(s32[2]{0:T(128)S(1)} %pad_add_fusion._.place, bf16[16,96,384]{2,1,0:T(8,128)(2,1)S(1)} %all_to_all.26.rows, bf16[8,96,256]{2,1,0:T(8,128)(2,1)S(1)} %all_to_all.25.cols, bf16[1536,768]{1,0:T(8,128)(2,1)S(1)} %bitcast.4), custom_call_target="tpu_custom_call" | custom-call | tf_op jit(solution)/shard_map/partial_totals/pallas_call | solution.py:205
  70.2 17.7 %all_to_all.27.arrived = bf16[32,32,96]{2,1,0:T(8,128)(2,1)S(1)} all-to-all(bf16[32,32,96]{2,1,0:T(8,128)(2,1)S(1)} %partial_totals.1), channel_id=1, replica_groups=mesh['gx'=8,'gy_0'=2,'gy_1'=8,'gz'=4] {'gx','gz'}, dimensions={0} | all-to-all | bytes 393216 | tf_op jit(solution)/shard_map/all_to_all | solution.py:24
  87.9 0.0 copy-done.2
  87.9 1.2 final_shares.1
  89.1 17.7 %all_to_all.28 = bf16[16,48,250]{2,1,0:T(8,128)(2,1)S(1)} all-to-all(bf16[16,48,250]{2,1,0:T(8,128)(2,1)S(1)} %final_shares.1), channel_id=1, replica_groups=mesh['gx'=8,'gy_0'=2,'gy_1'=8,'gz'=4] {'gy_0','gy_1'}, dimensions={0} | all-to-all | bytes 768000 | tf_op jit(solution)/shard_map/all_to_all | solution.py:24
  106.8 0.1 reduce_sum.21
  106.9 11.1 %all_to_all.29 = bf16[8,6,250]{2,1,0:T(8,128)(2,1)S(1)} all-to-all(bf16[8,6,250]{2,1,0:T(8,128)(2,1)S(1)} %reshape.11), channel_id=1, replica_groups=mesh['gx'=8,'gy_0'=2,'gy_1'=8,'gz'=4] {'gx'}, dimensions={0} | all-to-all | bytes 48000 | tf_op jit(solution)/shard_map/all_to_all | solution.py:24
  118.1 0.6 fusion
  (2 shorter events, 0.0 us)
Async XLA Ops:
  0.6 29.7 %copy-start = (bf16[1536,1,768]{2,0,1:T(8,128)(2,1)S(1)}, bf16[1536,1,768]{2,0,1:T(8,128)(2,1)}, u32[]{:S(2)}) copy-start(bf16[1536,1,768]{2,0,1:T(8,128)(2,1)} %param.5) | copy-start | bytes 7077892
  0.7 1.3 %copy-start.1 = (bf16[96,4000]{1,0:T(8,128)(2,1)S(1)}, bf16[96,4000]{1,0:T(8,128)(2,1)}, u32[]{:S(2)}) copy-start(bf16[96,4000]{1,0:T(8,128)(2,1)} %colloc.1) | copy-start | bytes 2304004
  2.0 1.6 %copy-start.3 = (bf16[4000,256]{1,0:T(8,128)(2,1)S(1)}, bf16[4000,256]{1,0:T(8,128)(2,1)}, u32[]{:S(2)}) copy-start(bf16[4000,256]{1,0:T(8,128)(2,1)} %coeffs_hbm.1) | copy-start | bytes 6144004
  68.0 19.9 %copy-start.2 = (bf16[96,4000]{1,0:T(8,128)(2,1)S(1)}, bf16[96,4000]{1,0:T(8,128)(2,1)}, u32[]{:S(2)}) copy-start(bf16[96,4000]{1,0:T(8,128)(2,1)} %colloc.1) | copy-start | bytes 2304004

commit v3 on v2

v3 whole, which is shorter than its diff:
```python
import functools

import jax
import jax.numpy as jnp
from jax import lax
from jax.experimental import pallas as pl
from jax.experimental.pallas import tpu as pltpu
from jax.sharding import Mesh
from jax.sharding import PartitionSpec as P

W = 96
LANES = 128
GRANT = 24 * 1024 * 1024
GY = ("gy_0", "gy_1")
GX_GY = ("gx", "gy_0", "gy_1")
BF16 = jnp.bfloat16
F32 = jnp.float32
IN_VMEM = pl.BlockSpec(memory_space=pltpu.VMEM)
IN_HBM = pl.BlockSpec(memory_space=pltpu.HBM)
IN_SMEM = pl.BlockSpec(memory_space=pltpu.SMEM)
PARAMS = pltpu.CompilerParams(vmem_limit_bytes=GRANT)


def exchange_pieces(pieces, axis):
    return lax.all_to_all(pieces, axis, split_axis=0, concat_axis=0, tiled=True)


def one_hot(shape, target):
    rows = lax.broadcasted_iota(jnp.int32, shape, 0)
    cols = lax.broadcasted_iota(jnp.int32, shape, 1)
    return jnp.where(cols == target(rows), 1.0, 0.0).astype(BF16)


def times(left, right, left_dim=1, right_dim=0):
    dims = (((left_dim,), (right_dim,)), ((), ()))
    return lax.dot_general(left, right, dims, preferred_element_type=F32)


def three_pieces(value):
    high = value.astype(BF16).astype(F32)
    middle = (value - high).astype(BF16).astype(F32)
    return high, middle, value - high - middle


def occupied(sizes, chunk, _, colloc_hbm, coeffs_hbm, copies, block, sums, colloc, coeffs, sems):
    size_x, size_z, per_rows = sizes
    width, group = coeffs.shape
    points = colloc.shape[0]
    starts = range(0, width, chunk)
    copies_in = []
    for k, at in enumerate(starts):
        part = pl.ds(at, min(chunk, width - at))
        copies_in.append(
            (
                pltpu.make_async_copy(colloc_hbm.at[:, part], colloc.at[:, part], sems.at[0, k]),
                pltpu.make_async_copy(coeffs_hbm.at[part, :], coeffs.at[part, :], sems.at[1, k]),
            )
        )
    for first, second in copies_in:
        first.start()
        second.start()
    acc = jnp.zeros((points, group), F32)
    for (first, second), at in zip(copies_in, starts):
        first.wait()
        second.wait()
        part = pl.ds(at, min(chunk, width - at))
        acc += times(colloc[:, part], coeffs[part, :])
    occ = acc.astype(BF16)
    vals = occ.astype(F32)
    density = jnp.sum(vals * vals, axis=1, keepdims=True).astype(BF16)
    square = one_hot((points, points), lambda rows: rows)
    density = times(jnp.broadcast_to(density, (points, LANES)), square, 0, 0)[: sums.shape[1]]
    own = size_x * per_rows

    def source(col):
        return ((col % own) // per_rows) * (size_z * per_rows) + (col // own) * per_rows + col % per_rows

    pick = one_hot((LANES, LANES), lambda rows: jnp.where(rows < W, source(rows), -1))
    window = times(colloc[:, :LANES], pick, 1, 1)
    block[:, :group] = occ
    block[:, group:] = window.astype(BF16)
    for a in range(size_x):
        sums[a] = density
        copies[a] = occ


def potential_rows(sums, block, core, copies, density):
    size_x, _, points = sums.shape
    size_y = copies.shape[0]
    group = block.shape[1] - LANES
    for a in range(size_x):
        density[:, a * points : (a + 1) * points] = sums[a]
    right = jnp.broadcast_to(density[:1, :], (LANES, size_x * points)).astype(BF16)
    lane = lax.broadcasted_iota(jnp.int32, (points, LANES), 1)
    occ = block[:, :group]
    window = block[:, group:].astype(F32)
    halves = core.shape[0] // (size_y * points)
    for y in range(size_y):
        tail = window
        for half in range(halves):
            share = times(core[pl.ds((half * size_y + y) * points, points), :], right, 1, 1)
            for k, piece in enumerate(three_pieces(share)):
                tail = jnp.where(lane == W + 3 * half + k, piece, tail)
        copies[y, :, :group] = occ
        copies[y, :, group:] = tail.astype(BF16)


def add_rows(per_step, rows, half, right, core, totals, tails):
    size_y, points, _ = rows.shape
    group = right.shape[1]
    height = per_step * points
    for y in range(0, size_y, per_step):
        left = rows[pl.ds(y, per_step), :, :group].reshape(height, group)
        tail = rows[pl.ds(y, per_step), :, group:].reshape(height, LANES)
        gram = times(left, right, 1, 1)
        at = pl.multiple_of(half * (size_y * points) + y * points, points)
        mixed = (core[pl.ds(at, height), :].astype(F32) * gram).astype(BF16)
        totals += times(tail, mixed, 0, 0)
        for step in range(per_step):
            tails += tail[step * points : (step + 1) * points].astype(F32)
    return totals, tails


def near_totals(per_step, place, near, cols, core, totals, tails):
    right = cols[...].reshape(-1, cols.shape[2])
    zeros = (jnp.zeros(totals.shape, F32), jnp.zeros(tails.shape, F32))
    totals[...], tails[...] = add_rows(per_step, near, place[2], right, core, *zeros)


def partial_totals(sizes, per_step, place, totals, tails, far, cols, core, sent, stored):
    size_x, size_z, per_rows = sizes
    points = far.shape[1]
    own = size_x * per_rows
    right = cols[...].reshape(-1, cols.shape[2])
    totals, tails = add_rows(per_step, far, 1 - place[2], right, core, totals[...], tails[...])
    lane = lax.broadcasted_iota(jnp.int32, (points, LANES), 1)
    first = W + 3 * place[2]
    kept = (lane >= first) & (lane < first + 3)
    share = jnp.sum(jnp.where(kept, tails, 0.0), axis=1, keepdims=True)
    per_row = points // own
    point = lax.broadcasted_iota(jnp.int32, (points, LANES), 0)
    behind = W + 3 * (point % per_row)
    packed = jnp.zeros((points, LANES), F32)
    for k, piece in enumerate(three_pieces(share)):
        packed = jnp.where(lane == behind + k, piece, packed)
    fold_row = lax.broadcasted_iota(jnp.int32, (own, points), 0)
    fold_col = lax.broadcasted_iota(jnp.int32, (own, points), 1)
    fold = jnp.where(fold_col // per_row == fold_row, 1.0, 0.0).astype(BF16)
    packed = times(fold, packed.astype(BF16))
    stored[:, : size_x * points] = totals
    lane = lax.broadcasted_iota(jnp.int32, (LANES, LANES), 1)
    for a in range(size_x):
        start = a * points // LANES * LANES
        shift = a * points - start
        found = stored[:, pl.ds(start, 2 * LANES)]
        if shift:
            found = pltpu.roll(found, 2 * LANES - shift, 1)
        found = jnp.where(lane < points, found[:, :LANES], 0.0)
        carried = jnp.where(place[0] == a, packed, 0.0)
        for g in range(size_z):
            sent[a * size_z + g] = (found[g * own : (g + 1) * own] + carried).astype(BF16)


def final_shares(sizes, place, arrived, block, colloc, shares, rows):
    size_x, _, per_rows = sizes
    size_y, height, part = shares.shape
    points = block.shape[0]
    own = size_x * per_rows
    per_row = points // own
    total = jnp.sum(arrived[...].astype(F32), axis=0)
    unfold_row = lax.broadcasted_iota(jnp.int32, (points, own), 0)
    unfold_col = lax.broadcasted_iota(jnp.int32, (points, own), 1)
    unfold = jnp.where(unfold_row // per_row == unfold_col, 1.0, 0.0).astype(BF16)
    spread_out = jnp.zeros((points, LANES), F32)
    for piece in three_pieces(total):
        spread_out += times(unfold, piece.astype(BF16))
    lane = lax.broadcasted_iota(jnp.int32, (points, LANES), 1)
    behind = W + 3 * (lax.broadcasted_iota(jnp.int32, (points, LANES), 0) % per_row)
    kept = (lane >= behind) & (lane < behind + 3)
    potential = jnp.sum(jnp.where(kept, spread_out, 0.0), axis=1, keepdims=True)
    window = block[:, block.shape[1] - LANES :]
    pick = one_hot((own, LANES), lambda row: row + place[1] * own)
    weighted = (times(window, pick, 1, 1) * potential).astype(BF16)

    def spread(which):
        def target(row):
            inside = row % (2 * per_rows)
            found = (row // (2 * per_rows)) * per_rows + inside % per_rows
            return jnp.where(inside // per_rows == which, found, -1)

        return one_hot((height, own), target)

    left = times(spread(0), weighted, 1, 1) + times(spread(1), total[:, :points].astype(BF16))
    rows[:, : colloc.shape[1]] = times(left.astype(BF16), colloc[...])
    for c in range(size_y):
        start = (c * part) // LANES * LANES
        span = -(-(c * part + part - start) // LANES) * LANES
        found = rows[:, pl.ds(start, span)]
        shift = c * part - start
        if shift:
            found = pltpu.roll(found, span - shift, 1)
        shares[c] = found[:, :part].astype(BF16)


def work(colloc, occ_coeffs, core):
    points, width = colloc.shape
    group = occ_coeffs.shape[1]
    size_x = lax.axis_size("gx")
    near_y = lax.axis_size("gy_1")
    size_y = lax.axis_size(GY)
    size_z = lax.axis_size("gz")
    row_count = core.shape[0]
    flat_cols = core.shape[2]
    per_rows = W // (size_x * size_z)
    own = size_x * per_rows
    part = width // size_y
    sizes = (size_x, size_z, per_rows)
    core_flat = core.reshape(row_count, flat_cols)
    place = jnp.stack([lax.axis_index("gx"), lax.axis_index("gz"), lax.axis_index("gy_0")])
    place = place.astype(jnp.int32)
    chunk = 8 * LANES
    steps = -(-width // chunk)

    copies, block, sums = pl.pallas_call(
        functools.partial(occupied, sizes, chunk),
        in_specs=[IN_SMEM, IN_HBM, IN_HBM],
        out_specs=[IN_VMEM, IN_VMEM, IN_VMEM],
        out_shape=[
            jax.ShapeDtypeStruct((size_x, points, group), BF16),
            jax.ShapeDtypeStruct((points, group + LANES), BF16),
            jax.ShapeDtypeStruct((size_x, 8, points), F32),
        ],
        scratch_shapes=[
            pltpu.VMEM((points, width), BF16),
            pltpu.VMEM((width, group), BF16),
            pltpu.SemaphoreType.DMA((2, steps)),
        ],
        compiler_params=pltpu.CompilerParams(vmem_limit_bytes=53 * 1024 * 1024),
        name="occupied",
    )(place, colloc, occ_coeffs)
    sums = exchange_pieces(sums, "gx")

    row_copies = pl.pallas_call(
        potential_rows,
        in_specs=[IN_VMEM, IN_VMEM, IN_VMEM],
        out_specs=IN_VMEM,
        out_shape=jax.ShapeDtypeStruct((near_y, points, group + LANES), BF16),
        scratch_shapes=[pltpu.VMEM((8, flat_cols), F32)],
        compiler_params=PARAMS,
        name="potential_rows",
    )(sums, block, core_flat)
    near = exchange_pieces(row_copies, "gy_1")
    far = lax.ppermute(near, "gy_0", [(0, 1), (1, 0)])
    cols = exchange_pieces(copies, "gx")

    totals, tails = pl.pallas_call(
        functools.partial(near_totals, 4),
        in_specs=[IN_SMEM, IN_VMEM, IN_VMEM, IN_VMEM],
        out_specs=[IN_VMEM, IN_VMEM],
        out_shape=[
            jax.ShapeDtypeStruct((LANES, flat_cols), F32),
            jax.ShapeDtypeStruct((points, LANES), F32),
        ],
        compiler_params=PARAMS,
        name="near_totals",
    )(place, near, cols, core_flat)
    sent = pl.pallas_call(
        functools.partial(partial_totals, sizes, 4),
        in_specs=[IN_SMEM, IN_VMEM, IN_VMEM, IN_VMEM, IN_VMEM, IN_VMEM],
        out_specs=IN_VMEM,
        out_shape=jax.ShapeDtypeStruct((size_x * size_z, own, LANES), BF16),
        scratch_shapes=[pltpu.VMEM((LANES, flat_cols + LANES), F32)],
        compiler_params=PARAMS,
        name="partial_totals",
    )(place, totals, tails, far, cols, core_flat)
    arrived = exchange_pieces(sent, ("gx", "gz"))

    shares = pl.pallas_call(
        functools.partial(final_shares, sizes),
        in_specs=[IN_SMEM, IN_VMEM, IN_VMEM, IN_VMEM],
        out_specs=IN_VMEM,
        out_shape=jax.ShapeDtypeStruct((size_y, 2 * own, part), BF16),
        scratch_shapes=[pltpu.VMEM((2 * own, -(-width // LANES) * LANES), F32)],
        compiler_params=PARAMS,
        name="final_shares",
    )(place, arrived, block, colloc)
    both = exchange_pieces(shares, GY).astype(F32).sum(axis=0)
    both = both.astype(BF16).reshape(size_x, 2 * per_rows, part)
    both = exchange_pieces(both, "gx").astype(F32).sum(axis=0)
    return (both[:per_rows], both[per_rows:])


def solution(mesh):
    split = Mesh(
        mesh.devices.reshape(mesh.shape["gx"], 2, 8, mesh.shape["gz"]), ("gx", "gy_0", "gy_1", "gz")
    )
    return jax.shard_map(
        work,
        mesh=split,
        in_specs=(P(GX_GY, None), P(None, "gz"), P("gx", GY, None)),
        out_specs=(P(("gx", "gz"), GY), P(("gx", "gz"), GY)),
        check_vma=False,
    )
```

time: 119 us -> 118 us (level)
  blocking collectives: 108 us -> 91.5 us
  waiting for transfers between devices: 0 us -> 9.52 us
  starting transfers between devices: 0 us -> 5.9 us
  Pallas kernels: 6.28 us -> 9.25 us
  local copies, waits for them, and re-layouts: 3.48 us -> 0.64 us
    all_to_all x5, blocking collectives: 108 us -> 91.5 us  [exchange_pieces(): return lax.all_to_all(pieces, axis, split_axis=0, concat_axis=0, tiled=True)]
    all_to_all x0 -> x1, waiting for transfers between devices: none -> 9.35 us  [exchange_pieces(): return lax.all_to_all(pieces, axis, split_axis=0, concat_axis=0, tiled=True)]
    all_to_all x0 -> x1, starting transfers between devices: none -> 3.45 us  [exchange_pieces(): return lax.all_to_all(pieces, axis, split_axis=0, concat_axis=0, tiled=True)]
    pallas_call x4 -> x5, Pallas kernels: 6.28 us -> 9.25 us  [the longest x1 3.13 us: work(): pl.pallas_call(functools.partial(occupied, sizes, chunk), in_specs=[IN_SM...]
    unnamed x8 -> x6, local copies, waits for them, and re-layouts: 2.86 us -> 0.01 us
    ppermute x0 -> x1, starting transfers between devices: none -> 2.44 us  [work(): far = lax.ppermute(near, 'gy_0', [(0, 1), (1, 0)])]
  transfers between devices with their start and end apart: 0 -> 2, of which waited for: 0 -> 2; matrix products, arithmetic and copies ran while one was open for 0% -> 0% of each run, Pallas kernels for 0% -> 1%
where the time goes in v3:
time: 118 us
  blocking collectives  91.5 us (78%)
  waiting for transfers between devices  9.52 us (8%)
  Pallas kernels  9.25 us (8%)
  starting transfers between devices  5.9 us (5%)
    all_to_all x5, blocking collectives, exchange_pieces(): return lax.all_to_all(pieces, axis, split_axis=0, concat_axis=0, tiled=True)  91.5 us
    all_to_all x1, waiting for transfers between devices, exchange_pieces(): return lax.all_to_all(pieces, axis, split_axis=0, concat_axis=0, tiled=True)  9.35 us
    all_to_all x1, starting transfers between devices, exchange_pieces(): return lax.all_to_all(pieces, axis, split_axis=0, concat_axis=0, tiled=True)  3.45 us
    pallas_call x1, Pallas kernels, work(): pl.pallas_call(functools.partial(occupied, sizes, chunk), in_specs=[IN_SM...  3.13 us
    ppermute x1, starting transfers between devices, work(): far = lax.ppermute(near, 'gy_0', [(0, 1), (1, 0)])  2.44 us
  transfers between devices with their start and end apart: 2, of which 2 were waited for; matrix products, arithmetic and copies ran while one was open for 0% of the time, Pallas kernels for 1%

profile of v3, /device:TPU:10, one launch (start us, length us, event | category | flops | bytes accessed | tf_op | source)
XLA Modules:
  0.0 117.7 jit_solution(6859337532677221355)
XLA Ops:
  0.6 0.0 copy-start
  0.6 0.1 pad_add_fusion._.place
  0.7 3.1 %occupied.1 = (bf16[8,96,256]{2,1,0:T(8,128)(2,1)S(1)}, bf16[96,384]{1,0:T(8,128)(2,1)S(1)}, f32[8,8,96]{2,1,0:T(8,128)S(1)}) custom-call(s32[3]{0:T(128)S(1)} %pad_add_fusion._.place, bf16[96,4000]{1,0:T(8,128)(2,1)} %colloc.1, bf16[4000,256]{1,0:T(8,128)(2,1)} %coeffs_hbm.1), custom_call_target="tpu_custom_call" | custom-call | tf_op jit(solution)/shard_map/occupied/pallas_call | solution.py:224
  3.9 0.0 copy-start.2
  3.9 18.1 %all_to_all.30.sums = f32[8,8,96]{2,1,0:T(8,128)S(1)} all-to-all(f32[8,8,96]{2,1,0:T(8,128)S(1)} %get-tuple-element.7), channel_id=1, replica_groups=mesh['gx'=8,'gy_0'=2,'gy_1'=8,'gz'=4] {'gx'}, dimensions={0} | all-to-all | bytes 49152 | tf_op jit(solution)/shard_map/all_to_all | solution.py:25
  22.0 0.0 copy-done
  22.0 1.2 %potential_rows.1 = bf16[8,96,384]{2,1,0:T(8,128)(2,1)S(1)} custom-call(f32[8,8,96]{2,1,0:T(8,128)S(1)} %all_to_all.30.sums, bf16[96,384]{1,0:T(8,128)(2,1)S(1)} %get-tuple-element.8.block, bf16[1536,768]{1,0:T(8,128)(2,1)S(1)} %bitcast.4), custom_call_target="tpu_custom_call" | custom-call | tf_op jit(solution)/shard_map/potential_rows/pallas_call | solution.py:243
  23.2 23.4 %all_to_all.31.near = bf16[8,96,384]{2,1,0:T(8,128)(2,1)S(1)} all-to-all(bf16[8,96,384]{2,1,0:T(8,128)(2,1)S(1)} %potential_rows.1), channel_id=1, replica_groups=mesh['gx'=8,'gy_0'=2,'gy_1'=8,'gz'=4] {'gy_1'}, dimensions={0} | all-to-all | bytes 1179648 | tf_op jit(solution)/shard_map/all_to_all | solution.py:25
  46.6 0.0 copy-done.2
  46.6 3.5 %all-to-all-start.2 = ((bf16[8,96,256]{2,1,0:T(8,128)(2,1)}), bf16[8,96,256]{2,1,0:T(8,128)(2,1)S(1)}, u32[]{:S(2)}, u32[]{:S(2)}) async-start(bf16[8,96,256]{2,1,0:T(8,128)(2,1)} %copy-done.2), calls=%async_computation.2 | async-start | bytes 786432 | tf_op jit(solution)/shard_map/all_to_all | solution.py:25
  50.1 2.4 %collective-permute-start = (bf16[8,96,384]{2,1,0:T(8,128)(2,1)S(1)}, bf16[8,96,384]{2,1,0:T(8,128)(2,1)}, u32[]{:S(2)}, u32[]{:S(2)}) collective-permute-start(bf16[8,96,384]{2,1,0:T(8,128)(2,1)S(1)} %all_to_all.31.near), channel_id=1, source_target_pairs={{0,32},{32,0},{1,33},{33,1},{2,34},{34,2},{3,35},{35,3},{4,36},{36... | collective-permute-start | bytes 1769480 | tf_op jit(solution)/shard_map/ppermute | solution.py:253
  52.5 9.3 %all-to-all-done.2.cols = bf16[8,96,256]{2,1,0:T(8,128)(2,1)S(1)} async-done(((bf16[8,96,256]{2,1,0:T(8,128)(2,1)}), bf16[8,96,256]{2,1,0:T(8,128)(2,1)S(1)}, u32[]{:S(2)}, u32[]{:S(2)}) %all-to-all-start.2) | async-done | bytes 393248 | tf_op jit(solution)/shard_map/all_to_all | solution.py:25
  61.9 1.4 %near_totals.1 = (f32[128,768]{1,0:T(8,128)S(1)}, f32[96,128]{1,0:T(8,128)S(1)}) custom-call(s32[3]{0:T(128)S(1)} %pad_add_fusion._.place, bf16[8,96,384]{2,1,0:T(8,128)(2,1)S(1)} %all_to_all.31.near, bf16[8,96,256]{2,1,0:T(8,128)(2,1)S(1)} %all-to-all-done.2.cols, bf16[1536,768]{1,0:T(8,128)(2,1)S(1)} %bitcast.5), custom_call_target="tpu_custom_call" | custom-call | tf_op jit(solution)/shard_map/near_totals/pallas_call | solution.py:256
  63.3 0.0 copy-start.1
  63.3 0.2 collective-permute-done.far
  63.4 2.2 %partial_totals.1 = bf16[32,24,128]{2,1,0:T(8,128)(2,1)S(1)} custom-call(s32[3]{0:T(128)S(1)} %pad_add_fusion._.place, f32[128,768]{1,0:T(8,128)S(1)} %get-tuple-element.10.totals, f32[96,128]{1,0:T(8,128)S(1)} %get-tuple-element.11.tails, bf16[8,96,384]{2,1,0:T(8,128)(2,1)} %collective-permute-done.far, bf16[8,96,256]{2,1,0:T(8,128)(2,1)S(1)} %all-to-all-done.2.cols, ...), custom_call_target="tpu_custom_call" | custom-call | tf_op jit(solution)/shard_map/partial_totals/pallas_call | solution.py:267
  65.7 20.4 %all_to_all.32.arrived = bf16[32,24,128]{2,1,0:T(8,128)(2,1)S(1)} all-to-all(bf16[32,24,128]{2,1,0:T(8,128)(2,1)S(1)} %partial_totals.1), channel_id=1, replica_groups=mesh['gx'=8,'gy_0'=2,'gy_1'=8,'gz'=4] {'gx','gz'}, dimensions={0} | all-to-all | bytes 393216 | tf_op jit(solution)/shard_map/all_to_all | solution.py:25
  86.0 0.0 copy-done.1
  86.0 1.3 %final_shares.1 = bf16[16,48,250]{2,1,0:T(8,128)(2,1)S(1)} custom-call(s32[3]{0:T(128)S(1)} %pad_add_fusion._.place, bf16[32,24,128]{2,1,0:T(8,128)(2,1)S(1)} %all_to_all.32.arrived, bf16[96,384]{1,0:T(8,128)(2,1)S(1)} %get-tuple-element.8.block, bf16[96,4000]{1,0:T(8,128)(2,1)S(1)} %copy-done.1), custom_call_target="tpu_custom_call" | custom-call | tf_op jit(solution)/shard_map/final_shares/pallas_call | solution.py:278
  87.3 18.9 %all_to_all.33 = bf16[16,48,250]{2,1,0:T(8,128)(2,1)S(1)} all-to-all(bf16[16,48,250]{2,1,0:T(8,128)(2,1)S(1)} %final_shares.1), channel_id=1, replica_groups=mesh['gx'=8,'gy_0'=2,'gy_1'=8,'gz'=4] {'gy_0','gy_1'}, dimensions={0} | all-to-all | bytes 768000 | tf_op jit(solution)/shard_map/all_to_all | solution.py:25
  106.2 0.1 reduce_sum.21
  106.3 10.8 %all_to_all.34 = bf16[8,6,250]{2,1,0:T(8,128)(2,1)S(1)} all-to-all(bf16[8,6,250]{2,1,0:T(8,128)(2,1)S(1)} %reshape.11), channel_id=1, replica_groups=mesh['gx'=8,'gy_0'=2,'gy_1'=8,'gz'=4] {'gx'}, dimensions={0} | all-to-all | bytes 48000 | tf_op jit(solution)/shard_map/all_to_all | solution.py:25
  117.1 0.6 fusion
  (2 shorter events, 0.0 us)
Async XLA Ops:
  0.6 21.4 %copy-start = (bf16[1536,1,768]{2,0,1:T(8,128)(2,1)S(1)}, bf16[1536,1,768]{2,0,1:T(8,128)(2,1)}, u32[]{:S(2)}) copy-start(bf16[1536,1,768]{2,0,1:T(8,128)(2,1)} %param.5) | copy-start | bytes 7077892
  3.9 42.7 %copy-start.2 = (bf16[8,96,256]{2,1,0:T(8,128)(2,1)}, bf16[8,96,256]{2,1,0:T(8,128)(2,1)S(1)}, u32[]{:S(2)}) copy-start(bf16[8,96,256]{2,1,0:T(8,128)(2,1)S(1)} %get-tuple-element.9) | copy-start | bytes 1179652
  46.6 15.3 %all-to-all-start.2 = ((bf16[8,96,256]{2,1,0:T(8,128)(2,1)}), bf16[8,96,256]{2,1,0:T(8,128)(2,1)S(1)}, u32[]{:S(2)}, u32[]{:S(2)}) async-start(bf16[8,96,256]{2,1,0:T(8,128)(2,1)} %copy-done.2), calls=%async_computation.2 | async-start | bytes 786432 | tf_op jit(solution)/shard_map/all_to_all | solution.py:25
  50.1 13.4 %collective-permute-start = (bf16[8,96,384]{2,1,0:T(8,128)(2,1)S(1)}, bf16[8,96,384]{2,1,0:T(8,128)(2,1)}, u32[]{:S(2)}, u32[]{:S(2)}) collective-permute-start(bf16[8,96,384]{2,1,0:T(8,128)(2,1)S(1)} %all_to_all.31.near), channel_id=1, source_target_pairs={{0,32},{32,0},{1,33},{33,1},{2,34},{34,2},{3,35},{35,3},{4,36},{36... | collective-permute-start | bytes 1769480 | tf_op jit(solution)/shard_map/ppermute | solution.py:253
  63.3 22.8 %copy-start.1 = (bf16[96,4000]{1,0:T(8,128)(2,1)S(1)}, bf16[96,4000]{1,0:T(8,128)(2,1)}, u32[]{:S(2)}) copy-start(bf16[96,4000]{1,0:T(8,128)(2,1)} %colloc.1) | copy-start | bytes 2304004

commit v4 on v3

--- a/solution.py
+++ b/solution.py
@@ -10,6 +10,7 @@
 
 W = 96
 LANES = 128
+SUBLANES = 8
 GRANT = 24 * 1024 * 1024
 GY = ("gy_0", "gy_1")
 GX_GY = ("gx", "gy_0", "gy_1")
@@ -163,7 +164,8 @@
 
 def final_shares(sizes, place, arrived, block, colloc, shares, rows):
     size_x, _, per_rows = sizes
-    size_y, height, part = shares.shape
+    pieces, pair, part = shares.shape
+    size_y = pieces // size_x
     points = block.shape[0]
     own = size_x * per_rows
     per_row = points // own
@@ -184,11 +186,11 @@
 
     def spread(which):
         def target(row):
-            inside = row % (2 * per_rows)
-            found = (row // (2 * per_rows)) * per_rows + inside % per_rows
+            inside = row % SUBLANES
+            found = (row // SUBLANES) * per_rows + inside % per_rows
             return jnp.where(inside // per_rows == which, found, -1)
 
-        return one_hot((height, own), target)
+        return one_hot((size_x * SUBLANES, own), target)
 
     left = times(spread(0), weighted, 1, 1) + times(spread(1), total[:, :points].astype(BF16))
     rows[:, : colloc.shape[1]] = times(left.astype(BF16), colloc[...])
@@ -199,7 +201,16 @@
         shift = c * part - start
         if shift:
             found = pltpu.roll(found, span - shift, 1)
-        shares[c] = found[:, :part].astype(BF16)
+        for a in range(size_x):
+            at = a * SUBLANES
+            shares[a * size_y + c] = found[at : at + pair, :part].astype(BF16)
+
+
+def outputs(arrived, coulomb, exchange):
+    per_rows = coulomb.shape[0]
+    total = jnp.sum(arrived[...].astype(F32), axis=0)
+    coulomb[...] = total[:per_rows]
+    exchange[...] = total[per_rows:]
 
 
 def work(colloc, occ_coeffs, core):
@@ -279,15 +290,20 @@
         functools.partial(final_shares, sizes),
         in_specs=[IN_SMEM, IN_VMEM, IN_VMEM, IN_VMEM],
         out_specs=IN_VMEM,
-        out_shape=jax.ShapeDtypeStruct((size_y, 2 * own, part), BF16),
-        scratch_shapes=[pltpu.VMEM((2 * own, -(-width // LANES) * LANES), F32)],
+        out_shape=jax.ShapeDtypeStruct((size_x * size_y, 2 * per_rows, part), BF16),
+        scratch_shapes=[pltpu.VMEM((size_x * SUBLANES, -(-width // LANES) * LANES), F32)],
         compiler_params=PARAMS,
         name="final_shares",
     )(place, arrived, block, colloc)
-    both = exchange_pieces(shares, GY).astype(F32).sum(axis=0)
-    both = both.astype(BF16).reshape(size_x, 2 * per_rows, part)
-    both = exchange_pieces(both, "gx").astype(F32).sum(axis=0)
-    return (both[:per_rows], both[per_rows:])
+    arrived = exchange_pieces(shares, GX_GY)
+    return pl.pallas_call(
+        outputs,
+        in_specs=[IN_VMEM],
+        out_specs=[IN_VMEM, IN_VMEM],
+        out_shape=[jax.ShapeDtypeStruct((per_rows, part), F32)] * 2,
+        compiler_params=PARAMS,
+        name="outputs",
+    )(arrived)
 
 
 def solution(mesh):

time: 118 us -> 118 us (level)
  the two profiles are of different devices: /device:TPU:10 before, /device:TPU:8 now
where the time goes in v4:
time: 118 us; the launch traced here: 117 us
  blocking collectives  91 us (77%)
  Pallas kernels  10 us (8%)
  waiting for transfers between devices  8.56 us (7%)
  starting transfers between devices  6.85 us (6%)
    all_to_all x4, blocking collectives, exchange_pieces(): return lax.all_to_all(pieces, axis, split_axis=0, concat_axis=0, tiled=True)  91 us
    all_to_all x1, waiting for transfers between devices, exchange_pieces(): return lax.all_to_all(pieces, axis, split_axis=0, concat_axis=0, tiled=True)  8.39 us
    all_to_all x1, starting transfers between devices, exchange_pieces(): return lax.all_to_all(pieces, axis, split_axis=0, concat_axis=0, tiled=True)  3.45 us
    ppermute x1, starting transfers between devices, work(): far = lax.ppermute(near, 'gy_0', [(0, 1), (1, 0)])  3.4 us
    pallas_call x1, Pallas kernels, work(): pl.pallas_call(functools.partial(occupied, sizes, chunk), in_specs=[IN_SM...  3.13 us
  transfers between devices with their start and end apart: 2, of which 2 were waited for; matrix products, arithmetic and copies ran while one was open for 0% of the time, Pallas kernels for 1%

profile of v4, /device:TPU:8, one launch (start us, length us, event | category | flops | bytes accessed | tf_op | source)
XLA Modules:
  0.0 117.2 jit_solution(14901487258160982193)
XLA Ops:
  0.6 0.0 copy-start
  0.6 0.1 pad_add_fusion._.place
  0.7 3.1 %occupied.1 = (bf16[8,96,256]{2,1,0:T(8,128)(2,1)S(1)}, bf16[96,384]{1,0:T(8,128)(2,1)S(1)}, f32[8,8,96]{2,1,0:T(8,128)S(1)}) custom-call(s32[3]{0:T(128)S(1)} %pad_add_fusion._.place, bf16[96,4000]{1,0:T(8,128)(2,1)} %colloc.1, bf16[4000,256]{1,0:T(8,128)(2,1)} %coeffs_hbm.1), custom_call_target="tpu_custom_call" | custom-call | tf_op jit(solution)/shard_map/occupied/pallas_call | solution.py:235
  3.9 0.0 copy-start.2
  3.9 18.1 %all_to_all.25.sums = f32[8,8,96]{2,1,0:T(8,128)S(1)} all-to-all(f32[8,8,96]{2,1,0:T(8,128)S(1)} %get-tuple-element.7), channel_id=1, replica_groups=mesh['gx'=8,'gy_0'=2,'gy_1'=8,'gz'=4] {'gx'}, dimensions={0} | all-to-all | bytes 49152 | tf_op jit(solution)/shard_map/all_to_all | solution.py:26
  22.0 0.0 copy-done
  22.0 1.2 %potential_rows.1 = bf16[8,96,384]{2,1,0:T(8,128)(2,1)S(1)} custom-call(f32[8,8,96]{2,1,0:T(8,128)S(1)} %all_to_all.25.sums, bf16[96,384]{1,0:T(8,128)(2,1)S(1)} %get-tuple-element.8.block, bf16[1536,768]{1,0:T(8,128)(2,1)S(1)} %bitcast.4), custom_call_target="tpu_custom_call" | custom-call | tf_op jit(solution)/shard_map/potential_rows/pallas_call | solution.py:254
  23.2 23.4 %all_to_all.26.near = bf16[8,96,384]{2,1,0:T(8,128)(2,1)S(1)} all-to-all(bf16[8,96,384]{2,1,0:T(8,128)(2,1)S(1)} %potential_rows.1), channel_id=1, replica_groups=mesh['gx'=8,'gy_0'=2,'gy_1'=8,'gz'=4] {'gy_1'}, dimensions={0} | all-to-all | bytes 1179648 | tf_op jit(solution)/shard_map/all_to_all | solution.py:26
  46.6 0.0 copy-done.2
  46.6 3.5 %all-to-all-start.2 = ((bf16[8,96,256]{2,1,0:T(8,128)(2,1)}), bf16[8,96,256]{2,1,0:T(8,128)(2,1)S(1)}, u32[]{:S(2)}, u32[]{:S(2)}) async-start(bf16[8,96,256]{2,1,0:T(8,128)(2,1)} %copy-done.2), calls=%async_computation.2 | async-start | bytes 786432 | tf_op jit(solution)/shard_map/all_to_all | solution.py:26
  50.1 3.4 %collective-permute-start = (bf16[8,96,384]{2,1,0:T(8,128)(2,1)S(1)}, bf16[8,96,384]{2,1,0:T(8,128)(2,1)}, u32[]{:S(2)}, u32[]{:S(2)}) collective-permute-start(bf16[8,96,384]{2,1,0:T(8,128)(2,1)S(1)} %all_to_all.26.near), channel_id=1, source_target_pairs={{0,32},{32,0},{1,33},{33,1},{2,34},{34,2},{3,35},{35,3},{4,36},{36... | collective-permute-start | bytes 1769480 | tf_op jit(solution)/shard_map/ppermute | solution.py:264
  53.5 8.4 %all-to-all-done.2.cols = bf16[8,96,256]{2,1,0:T(8,128)(2,1)S(1)} async-done(((bf16[8,96,256]{2,1,0:T(8,128)(2,1)}), bf16[8,96,256]{2,1,0:T(8,128)(2,1)S(1)}, u32[]{:S(2)}, u32[]{:S(2)}) %all-to-all-start.2) | async-done | bytes 393248 | tf_op jit(solution)/shard_map/all_to_all | solution.py:26
  61.9 1.4 %near_totals.1 = (f32[128,768]{1,0:T(8,128)S(1)}, f32[96,128]{1,0:T(8,128)S(1)}) custom-call(s32[3]{0:T(128)S(1)} %pad_add_fusion._.place, bf16[8,96,384]{2,1,0:T(8,128)(2,1)S(1)} %all_to_all.26.near, bf16[8,96,256]{2,1,0:T(8,128)(2,1)S(1)} %all-to-all-done.2.cols, bf16[1536,768]{1,0:T(8,128)(2,1)S(1)} %bitcast.5), custom_call_target="tpu_custom_call" | custom-call | tf_op jit(solution)/shard_map/near_totals/pallas_call | solution.py:267
  63.3 0.0 copy-start.1
  63.3 0.2 collective-permute-done.far
  63.4 2.2 %partial_totals.1 = bf16[32,24,128]{2,1,0:T(8,128)(2,1)S(1)} custom-call(s32[3]{0:T(128)S(1)} %pad_add_fusion._.place, f32[128,768]{1,0:T(8,128)S(1)} %get-tuple-element.10.totals, f32[96,128]{1,0:T(8,128)S(1)} %get-tuple-element.11.tails, bf16[8,96,384]{2,1,0:T(8,128)(2,1)} %collective-permute-done.far, bf16[8,96,256]{2,1,0:T(8,128)(2,1)S(1)} %all-to-all-done.2.cols, ...), custom_call_target="tpu_custom_call" | custom-call | tf_op jit(solution)/shard_map/partial_totals/pallas_call | solution.py:278
  65.7 21.3 %all_to_all.27.arrived = bf16[32,24,128]{2,1,0:T(8,128)(2,1)S(1)} all-to-all(bf16[32,24,128]{2,1,0:T(8,128)(2,1)S(1)} %partial_totals.1), channel_id=1, replica_groups=mesh['gx'=8,'gy_0'=2,'gy_1'=8,'gz'=4] {'gx','gz'}, dimensions={0} | all-to-all | bytes 393216 | tf_op jit(solution)/shard_map/all_to_all | solution.py:26
  87.0 0.0 copy-done.1
  87.0 1.4 %final_shares.1 = bf16[128,6,250]{2,1,0:T(8,128)(2,1)S(1)} custom-call(s32[3]{0:T(128)S(1)} %pad_add_fusion._.place, bf16[32,24,128]{2,1,0:T(8,128)(2,1)S(1)} %all_to_all.27.arrived, bf16[96,384]{1,0:T(8,128)(2,1)S(1)} %get-tuple-element.8.block, bf16[96,4000]{1,0:T(8,128)(2,1)S(1)} %copy-done.1), custom_call_target="tpu_custom_call" | custom-call | tf_op jit(solution)/shard_map/final_shares/pallas_call | solution.py:289
  88.4 28.1 %all_to_all.28.arrived = bf16[128,6,250]{2,1,0:T(8,128)(2,1)S(1)} all-to-all(bf16[128,6,250]{2,1,0:T(8,128)(2,1)S(1)} %final_shares.1), channel_id=1, replica_groups=mesh['gx'=8,'gy_0'=2,'gy_1'=8,'gz'=4] {'gx','gy_0','gy_1'}, dimensions={0} | all-to-all | bytes 768000 | tf_op jit(solution)/shard_map/all_to_all | solution.py:26
  116.5 0.7 outputs.1
Async XLA Ops:
  0.6 21.4 %copy-start = (bf16[1536,1,768]{2,0,1:T(8,128)(2,1)S(1)}, bf16[1536,1,768]{2,0,1:T(8,128)(2,1)}, u32[]{:S(2)}) copy-start(bf16[1536,1,768]{2,0,1:T(8,128)(2,1)} %param.5) | copy-start | bytes 7077892
  3.9 42.7 %copy-start.2 = (bf16[8,96,256]{2,1,0:T(8,128)(2,1)}, bf16[8,96,256]{2,1,0:T(8,128)(2,1)S(1)}, u32[]{:S(2)}) copy-start(bf16[8,96,256]{2,1,0:T(8,128)(2,1)S(1)} %get-tuple-element.9) | copy-start | bytes 1179652
  46.6 15.3 %all-to-all-start.2 = ((bf16[8,96,256]{2,1,0:T(8,128)(2,1)}), bf16[8,96,256]{2,1,0:T(8,128)(2,1)S(1)}, u32[]{:S(2)}, u32[]{:S(2)}) async-start(bf16[8,96,256]{2,1,0:T(8,128)(2,1)} %copy-done.2), calls=%async_computation.2 | async-start | bytes 786432 | tf_op jit(solution)/shard_map/all_to_all | solution.py:26
  50.1 13.4 %collective-permute-start = (bf16[8,96,384]{2,1,0:T(8,128)(2,1)S(1)}, bf16[8,96,384]{2,1,0:T(8,128)(2,1)}, u32[]{:S(2)}, u32[]{:S(2)}) collective-permute-start(bf16[8,96,384]{2,1,0:T(8,128)(2,1)S(1)} %all_to_all.26.near), channel_id=1, source_target_pairs={{0,32},{32,0},{1,33},{33,1},{2,34},{34,2},{3,35},{35,3},{4,36},{36... | collective-permute-start | bytes 1769480 | tf_op jit(solution)/shard_map/ppermute | solution.py:264
  63.3 23.7 %copy-start.1 = (bf16[96,4000]{1,0:T(8,128)(2,1)S(1)}, bf16[96,4000]{1,0:T(8,128)(2,1)}, u32[]{:S(2)}) copy-start(bf16[96,4000]{1,0:T(8,128)(2,1)} %colloc.1) | copy-start | bytes 2304004

commit v5 on v4

--- a/solution.py
+++ b/solution.py
@@ -85,7 +85,7 @@
         copies[a] = occ
 
 
-def potential_rows(sums, block, core, copies, density):
+def potential_rows(sums, block, core, copies, density, shares):
     size_x, _, points = sums.shape
     size_y = copies.shape[0]
     group = block.shape[1] - LANES
@@ -96,10 +96,13 @@
     occ = block[:, :group]
     window = block[:, group:].astype(F32)
     halves = core.shape[0] // (size_y * points)
+    for half in range(halves):
+        at = half * size_y * points
+        shares[pl.ds(at, size_y * points), :] = times(core[pl.ds(at, size_y * points), :], right, 1, 1)
     for y in range(size_y):
         tail = window
         for half in range(halves):
-            share = times(core[pl.ds((half * size_y + y) * points, points), :], right, 1, 1)
+            share = shares[pl.ds((half * size_y + y) * points, points), :]
             for k, piece in enumerate(three_pieces(share)):
                 tail = jnp.where(lane == W + 3 * half + k, piece, tail)
         copies[y, :, :group] = occ
@@ -122,18 +125,19 @@
     return totals, tails
 
 
-def near_totals(per_step, place, near, cols, core, totals, tails):
-    right = cols[...].reshape(-1, cols.shape[2])
-    zeros = (jnp.zeros(totals.shape, F32), jnp.zeros(tails.shape, F32))
-    totals[...], tails[...] = add_rows(per_step, near, place[2], right, core, *zeros)
-
-
-def partial_totals(sizes, per_step, place, totals, tails, far, cols, core, sent, stored):
+def after(cols, mark):
+    mark[...] = cols[0, :SUBLANES, :LANES].astype(F32)
+
+
+def partial_totals(sizes, per_step, place, _, near, far, cols, core, sent, stored):
     size_x, size_z, per_rows = sizes
     points = far.shape[1]
     own = size_x * per_rows
     right = cols[...].reshape(-1, cols.shape[2])
-    totals, tails = add_rows(per_step, far, 1 - place[2], right, core, totals[...], tails[...])
+    totals = jnp.zeros((LANES, right.shape[0]), F32)
+    tails = jnp.zeros((points, LANES), F32)
+    totals, tails = add_rows(per_step, near, place[2], right, core, totals, tails)
+    totals, tails = add_rows(per_step, far, 1 - place[2], right, core, totals, tails)
     lane = lax.broadcasted_iota(jnp.int32, (points, LANES), 1)
     first = W + 3 * place[2]
     kept = (lane >= first) & (lane < first + 3)
@@ -164,8 +168,10 @@
 
 def final_shares(sizes, place, arrived, block, colloc, shares, rows):
     size_x, _, per_rows = sizes
-    pieces, pair, part = shares.shape
+    pieces, _, lanes = shares.shape
+    wide = lanes // per_rows
     size_y = pieces // size_x
+    part = colloc.shape[1] // size_y
     points = block.shape[0]
     own = size_x * per_rows
     per_row = points // own
@@ -187,30 +193,35 @@
     def spread(which):
         def target(row):
             inside = row % SUBLANES
-            found = (row // SUBLANES) * per_rows + inside % per_rows
-            return jnp.where(inside // per_rows == which, found, -1)
+            found = (row // SUBLANES) * per_rows + inside // 2
+            return jnp.where((inside % 2 == which) & (inside // 2 < per_rows), found, -1)
 
         return one_hot((size_x * SUBLANES, own), target)
 
     left = times(spread(0), weighted, 1, 1) + times(spread(1), total[:, :points].astype(BF16))
     rows[:, : colloc.shape[1]] = times(left.astype(BF16), colloc[...])
     for c in range(size_y):
-        start = (c * part) // LANES * LANES
-        span = -(-(c * part + part - start) // LANES) * LANES
+        start = c * part // LANES * LANES
+        span = wide + LANES
         found = rows[:, pl.ds(start, span)]
         shift = c * part - start
         if shift:
             found = pltpu.roll(found, span - shift, 1)
+        found = found[:, :wide].astype(BF16)
         for a in range(size_x):
-            at = a * SUBLANES
-            shares[a * size_y + c] = found[at : at + pair, :part].astype(BF16)
+            for b in range(per_rows):
+                at = a * SUBLANES + 2 * b
+                shares[a * size_y + c, :, b * wide : (b + 1) * wide] = found[at : at + 2]
 
 
 def outputs(arrived, coulomb, exchange):
-    per_rows = coulomb.shape[0]
+    per_rows, part = coulomb.shape
+    wide = arrived.shape[2] // per_rows
     total = jnp.sum(arrived[...].astype(F32), axis=0)
-    coulomb[...] = total[:per_rows]
-    exchange[...] = total[per_rows:]
+    for b in range(per_rows):
+        at = b * wide
+        coulomb[b : b + 1] = total[:1, at : at + part]
+        exchange[b : b + 1] = total[1:, at : at + part]
 
 
 def work(colloc, occ_coeffs, core):
@@ -225,6 +236,7 @@
     per_rows = W // (size_x * size_z)
     own = size_x * per_rows
     part = width // size_y
+    wide = -(-part // LANES) * LANES
     sizes = (size_x, size_z, per_rows)
     core_flat = core.reshape(row_count, flat_cols)
     place = jnp.stack([lax.axis_index("gx"), lax.axis_index("gz"), lax.axis_index("gy_0")])
@@ -256,7 +268,7 @@
         in_specs=[IN_VMEM, IN_VMEM, IN_VMEM],
         out_specs=IN_VMEM,
         out_shape=jax.ShapeDtypeStruct((near_y, points, group + LANES), BF16),
-        scratch_shapes=[pltpu.VMEM((8, flat_cols), F32)],
+        scratch_shapes=[pltpu.VMEM((8, flat_cols), F32), pltpu.VMEM((row_count, LANES), F32)],
         compiler_params=PARAMS,
         name="potential_rows",
     )(sums, block, core_flat)
@@ -264,17 +276,14 @@
     far = lax.ppermute(near, "gy_0", [(0, 1), (1, 0)])
     cols = exchange_pieces(copies, "gx")
 
-    totals, tails = pl.pallas_call(
-        functools.partial(near_totals, 4),
-        in_specs=[IN_SMEM, IN_VMEM, IN_VMEM, IN_VMEM],
-        out_specs=[IN_VMEM, IN_VMEM],
-        out_shape=[
-            jax.ShapeDtypeStruct((LANES, flat_cols), F32),
-            jax.ShapeDtypeStruct((points, LANES), F32),
-        ],
-        compiler_params=PARAMS,
-        name="near_totals",
-    )(place, near, cols, core_flat)
+    mark = pl.pallas_call(
+        after,
+        in_specs=[IN_VMEM],
+        out_specs=IN_VMEM,
+        out_shape=jax.ShapeDtypeStruct((SUBLANES, LANES), F32),
+        compiler_params=PARAMS,
+        name="after",
+    )(cols)
     sent = pl.pallas_call(
         functools.partial(partial_totals, sizes, 4),
         in_specs=[IN_SMEM, IN_VMEM, IN_VMEM, IN_VMEM, IN_VMEM, IN_VMEM],
@@ -283,15 +292,15 @@
         scratch_shapes=[pltpu.VMEM((LANES, flat_cols + LANES), F32)],
         compiler_params=PARAMS,
         name="partial_totals",
-    )(place, totals, tails, far, cols, core_flat)
+    )(place, mark, near, far, cols, core_flat)
     arrived = exchange_pieces(sent, ("gx", "gz"))
 
     shares = pl.pallas_call(
         functools.partial(final_shares, sizes),
         in_specs=[IN_SMEM, IN_VMEM, IN_VMEM, IN_VMEM],
         out_specs=IN_VMEM,
-        out_shape=jax.ShapeDtypeStruct((size_x * size_y, 2 * per_rows, part), BF16),
-        scratch_shapes=[pltpu.VMEM((size_x * SUBLANES, -(-width // LANES) * LANES), F32)],
+        out_shape=jax.ShapeDtypeStruct((size_x * size_y, 2, per_rows * wide), BF16),
+        scratch_shapes=[pltpu.VMEM((size_x * SUBLANES, (width // LANES + 2) * LANES), F32)],
         compiler_params=PARAMS,
         name="final_shares",
     )(place, arrived, block, colloc)

time: 118 us -> 115 us (0.975)
  blocking collectives: 91 us -> 88.3 us
  waiting for transfers between devices: 8.56 us -> 10.1 us
    all_to_all x4, blocking collectives: 91 us -> 88.3 us  [exchange_pieces(): return lax.all_to_all(pieces, axis, split_axis=0, concat_axis=0, tiled=True)]
    ppermute x1, waiting for transfers between devices: 0.17 us -> 1.69 us  [work(): far = lax.ppermute(near, 'gy_0', [(0, 1), (1, 0)])]
    pallas_call x1, Pallas kernels: 1.4 us -> 0.01 us  [work(): pl.pallas_call(after, in_specs=[IN_VMEM], out_specs=IN_VMEM, out_shape=ja...]
  transfers between devices with their start and end apart: 2 -> 2, of which waited for: 2 -> 2; matrix products, arithmetic and copies ran while one was open for 0% -> 0% of each run, Pallas kernels for 1% -> 0%
where the time goes in v5:
time: 115 us
  blocking collectives  88.3 us (77%)
  waiting for transfers between devices  10.1 us (9%)
  Pallas kernels  9.08 us (8%)
  starting transfers between devices  6.85 us (6%)
    all_to_all x4, blocking collectives, exchange_pieces(): return lax.all_to_all(pieces, axis, split_axis=0, concat_axis=0, tiled=True)  88.3 us
    all_to_all x1, waiting for transfers between devices, exchange_pieces(): return lax.all_to_all(pieces, axis, split_axis=0, concat_axis=0, tiled=True)  8.4 us
    all_to_all x1, starting transfers between devices, exchange_pieces(): return lax.all_to_all(pieces, axis, split_axis=0, concat_axis=0, tiled=True)  3.45 us
    ppermute x1, starting transfers between devices, work(): far = lax.ppermute(near, 'gy_0', [(0, 1), (1, 0)])  3.39 us
    pallas_call x1, Pallas kernels, work(): pl.pallas_call(functools.partial(occupied, sizes, chunk), in_specs=[IN_SM...  3.13 us
    pallas_call x1, Pallas kernels, work(): pl.pallas_call(functools.partial(partial_totals, sizes, 4), in_specs=[IN_...  2.7 us
  transfers between devices with their start and end apart: 2, of which 2 were waited for; matrix products, arithmetic and copies ran while one was open for 0% of the time, Pallas kernels for 0%

profile of v5, /device:TPU:8, one launch (start us, length us, event | category | flops | bytes accessed | tf_op | source)
XLA Modules:
  0.0 115.1 jit_solution(8515990391343005835)
XLA Ops:
  0.6 0.0 copy-start
  0.6 0.1 pad_add_fusion._.place
  0.7 3.1 %occupied.1 = (bf16[8,96,256]{2,1,0:T(8,128)(2,1)S(1)}, bf16[96,384]{1,0:T(8,128)(2,1)S(1)}, f32[8,8,96]{2,1,0:T(8,128)S(1)}) custom-call(s32[3]{0:T(128)S(1)} %pad_add_fusion._.place, bf16[96,4000]{1,0:T(8,128)(2,1)} %colloc.1, bf16[4000,256]{1,0:T(8,128)(2,1)} %coeffs_hbm.1), custom_call_target="tpu_custom_call" | custom-call | tf_op jit(solution)/shard_map/occupied/pallas_call | solution.py:247
  3.9 0.0 copy-start.2
  3.9 18.1 %all_to_all.25.sums = f32[8,8,96]{2,1,0:T(8,128)S(1)} all-to-all(f32[8,8,96]{2,1,0:T(8,128)S(1)} %get-tuple-element.6), channel_id=1, replica_groups=mesh['gx'=8,'gy_0'=2,'gy_1'=8,'gz'=4] {'gx'}, dimensions={0} | all-to-all | bytes 49152 | tf_op jit(solution)/shard_map/all_to_all | solution.py:26
  22.0 0.0 copy-done
  22.0 0.9 potential_rows.1
  22.9 23.4 %all_to_all.26.near = bf16[8,96,384]{2,1,0:T(8,128)(2,1)S(1)} all-to-all(bf16[8,96,384]{2,1,0:T(8,128)(2,1)S(1)} %potential_rows.1), channel_id=1, replica_groups=mesh['gx'=8,'gy_0'=2,'gy_1'=8,'gz'=4] {'gy_1'}, dimensions={0} | all-to-all | bytes 1179648 | tf_op jit(solution)/shard_map/all_to_all | solution.py:26
  46.3 0.0 copy-done.2
  46.3 3.5 %all-to-all-start = ((bf16[8,96,256]{2,1,0:T(8,128)(2,1)}), bf16[8,96,256]{2,1,0:T(8,128)(2,1)S(1)}, u32[]{:S(2)}, u32[]{:S(2)}) async-start(bf16[8,96,256]{2,1,0:T(8,128)(2,1)} %copy-done.2), calls=%async_computation | async-start | bytes 786432 | tf_op jit(solution)/shard_map/all_to_all | solution.py:26
  49.7 3.4 %collective-permute-start = (bf16[8,96,384]{2,1,0:T(8,128)(2,1)S(1)}, bf16[8,96,384]{2,1,0:T(8,128)(2,1)}, u32[]{:S(2)}, u32[]{:S(2)}) collective-permute-start(bf16[8,96,384]{2,1,0:T(8,128)(2,1)S(1)} %all_to_all.26.near), channel_id=1, source_target_pairs={{0,32},{32,0},{1,33},{33,1},{2,34},{34,2},{3,35},{35,3},{4,36},{36... | collective-permute-start | bytes 1769480 | tf_op jit(solution)/shard_map/ppermute | solution.py:276
  53.1 8.4 %all-to-all-done.cols = bf16[8,96,256]{2,1,0:T(8,128)(2,1)S(1)} async-done(((bf16[8,96,256]{2,1,0:T(8,128)(2,1)}), bf16[8,96,256]{2,1,0:T(8,128)(2,1)S(1)}, u32[]{:S(2)}, u32[]{:S(2)}) %all-to-all-start) | async-done | bytes 393248 | tf_op jit(solution)/shard_map/all_to_all | solution.py:26
  61.5 0.0 copy-start.1
  61.5 1.7 %collective-permute-done.far = bf16[8,96,384]{2,1,0:T(8,128)(2,1)} collective-permute-done((bf16[8,96,384]{2,1,0:T(8,128)(2,1)S(1)}, bf16[8,96,384]{2,1,0:T(8,128)(2,1)}, u32[]{:S(2)}, u32[]{:S(2)}) %collective-permute-start) | collective-permute-done | bytes 589856 | tf_op jit(solution)/shard_map/ppermute | solution.py:276
  63.2 2.7 %partial_totals.1 = bf16[32,24,128]{2,1,0:T(8,128)(2,1)S(1)} custom-call(s32[3]{0:T(128)S(1)} %pad_add_fusion._.place, f32[8,128]{1,0:T(8,128)S(1)} %after.1._, bf16[8,96,384]{2,1,0:T(8,128)(2,1)S(1)} %all_to_all.26.near, bf16[8,96,384]{2,1,0:T(8,128)(2,1)} %collective-permute-done.far, bf16[8,96,256]{2,1,0:T(8,128)(2,1)S(1)} %all-to-all-done.cols, ...), custom_call_target="tpu_custom_call" | custom-call | tf_op jit(solution)/shard_map/partial_totals/pallas_call | solution.py:287
  65.9 21.3 %all_to_all.27.arrived = bf16[32,24,128]{2,1,0:T(8,128)(2,1)S(1)} all-to-all(bf16[32,24,128]{2,1,0:T(8,128)(2,1)S(1)} %partial_totals.1), channel_id=1, replica_groups=mesh['gx'=8,'gy_0'=2,'gy_1'=8,'gz'=4] {'gx','gz'}, dimensions={0} | all-to-all | bytes 393216 | tf_op jit(solution)/shard_map/all_to_all | solution.py:26
  87.2 0.0 copy-done.1
  87.2 1.4 %final_shares.1 = bf16[128,2,768]{2,1,0:T(2,128)(2,1)S(1)} custom-call(s32[3]{0:T(128)S(1)} %pad_add_fusion._.place, bf16[32,24,128]{2,1,0:T(8,128)(2,1)S(1)} %all_to_all.27.arrived, bf16[96,384]{1,0:T(8,128)(2,1)S(1)} %get-tuple-element.7.block, bf16[96,4000]{1,0:T(8,128)(2,1)S(1)} %copy-done.1), custom_call_target="tpu_custom_call" | custom-call | tf_op jit(solution)/shard_map/final_shares/pallas_call | solution.py:298
  88.6 25.5 %all_to_all.28.arrived = bf16[128,2,768]{2,1,0:T(2,128)(2,1)S(1)} all-to-all(bf16[128,2,768]{2,1,0:T(2,128)(2,1)S(1)} %final_shares.1), channel_id=1, replica_groups=mesh['gx'=8,'gy_0'=2,'gy_1'=8,'gz'=4] {'gx','gy_0','gy_1'}, dimensions={0} | all-to-all | bytes 786432 | tf_op jit(solution)/shard_map/all_to_all | solution.py:26
  114.1 1.0 outputs.1
  (1 shorter events, 0.0 us)
Async XLA Ops:
  0.6 21.4 %copy-start = (bf16[1536,1,768]{2,0,1:T(8,128)(2,1)S(1)}, bf16[1536,1,768]{2,0,1:T(8,128)(2,1)}, u32[]{:S(2)}) copy-start(bf16[1536,1,768]{2,0,1:T(8,128)(2,1)} %param.5) | copy-start | bytes 7077892
  3.9 42.4 %copy-start.2 = (bf16[8,96,256]{2,1,0:T(8,128)(2,1)}, bf16[8,96,256]{2,1,0:T(8,128)(2,1)S(1)}, u32[]{:S(2)}) copy-start(bf16[8,96,256]{2,1,0:T(8,128)(2,1)S(1)} %get-tuple-element.5) | copy-start | bytes 1179652
  46.3 15.3 %all-to-all-start = ((bf16[8,96,256]{2,1,0:T(8,128)(2,1)}), bf16[8,96,256]{2,1,0:T(8,128)(2,1)S(1)}, u32[]{:S(2)}, u32[]{:S(2)}) async-start(bf16[8,96,256]{2,1,0:T(8,128)(2,1)} %copy-done.2), calls=%async_computation | async-start | bytes 786432 | tf_op jit(solution)/shard_map/all_to_all | solution.py:26
  49.7 13.5 %collective-permute-start = (bf16[8,96,384]{2,1,0:T(8,128)(2,1)S(1)}, bf16[8,96,384]{2,1,0:T(8,128)(2,1)}, u32[]{:S(2)}, u32[]{:S(2)}) collective-permute-start(bf16[8,96,384]{2,1,0:T(8,128)(2,1)S(1)} %all_to_all.26.near), channel_id=1, source_target_pairs={{0,32},{32,0},{1,33},{33,1},{2,34},{34,2},{3,35},{35,3},{4,36},{36... | collective-permute-start | bytes 1769480 | tf_op jit(solution)/shard_map/ppermute | solution.py:276
  61.5 25.7 %copy-start.1 = (bf16[96,4000]{1,0:T(8,128)(2,1)S(1)}, bf16[96,4000]{1,0:T(8,128)(2,1)}, u32[]{:S(2)}) copy-start(bf16[96,4000]{1,0:T(8,128)(2,1)} %colloc.1) | copy-start | bytes 2304004

commit v6 on v5

--- a/solution.py
+++ b/solution.py
@@ -37,10 +37,12 @@
     return lax.dot_general(left, right, dims, preferred_element_type=F32)
 
 
-def three_pieces(value):
+PIECES = 2
+
+
+def in_pieces(value):
     high = value.astype(BF16).astype(F32)
-    middle = (value - high).astype(BF16).astype(F32)
-    return high, middle, value - high - middle
+    return high, value - high
 
 
 def occupied(sizes, chunk, _, colloc_hbm, coeffs_hbm, copies, block, sums, colloc, coeffs, sems):
@@ -60,26 +62,26 @@
     for first, second in copies_in:
         first.start()
         second.start()
+    own = size_x * per_rows
+
+    def source(col):
+        return ((col % own) // per_rows) * (size_z * per_rows) + (col // own) * per_rows + col % per_rows
+
+    pick = one_hot((LANES, LANES), lambda rows: jnp.where(rows < W, source(rows), -1))
+    square = one_hot((points, points), lambda rows: rows)
     acc = jnp.zeros((points, group), F32)
     for (first, second), at in zip(copies_in, starts):
         first.wait()
         second.wait()
         part = pl.ds(at, min(chunk, width - at))
         acc += times(colloc[:, part], coeffs[part, :])
+        if at == 0:
+            block[:, group:] = times(colloc[:, :LANES], pick, 1, 1).astype(BF16)
     occ = acc.astype(BF16)
     vals = occ.astype(F32)
     density = jnp.sum(vals * vals, axis=1, keepdims=True).astype(BF16)
-    square = one_hot((points, points), lambda rows: rows)
     density = times(jnp.broadcast_to(density, (points, LANES)), square, 0, 0)[: sums.shape[1]]
-    own = size_x * per_rows
-
-    def source(col):
-        return ((col % own) // per_rows) * (size_z * per_rows) + (col // own) * per_rows + col % per_rows
-
-    pick = one_hot((LANES, LANES), lambda rows: jnp.where(rows < W, source(rows), -1))
-    window = times(colloc[:, :LANES], pick, 1, 1)
     block[:, :group] = occ
-    block[:, group:] = window.astype(BF16)
     for a in range(size_x):
         sums[a] = density
         copies[a] = occ
@@ -103,8 +105,8 @@
         tail = window
         for half in range(halves):
             share = shares[pl.ds((half * size_y + y) * points, points), :]
-            for k, piece in enumerate(three_pieces(share)):
-                tail = jnp.where(lane == W + 3 * half + k, piece, tail)
+            for k, piece in enumerate(in_pieces(share)):
+                tail = jnp.where(lane == W + PIECES * half + k, piece, tail)
         copies[y, :, :group] = occ
         copies[y, :, group:] = tail.astype(BF16)
 
@@ -139,14 +141,14 @@
     totals, tails = add_rows(per_step, near, place[2], right, core, totals, tails)
     totals, tails = add_rows(per_step, far, 1 - place[2], right, core, totals, tails)
     lane = lax.broadcasted_iota(jnp.int32, (points, LANES), 1)
-    first = W + 3 * place[2]
-    kept = (lane >= first) & (lane < first + 3)
+    first = W + PIECES * place[2]
+    kept = (lane >= first) & (lane < first + PIECES)
     share = jnp.sum(jnp.where(kept, tails, 0.0), axis=1, keepdims=True)
     per_row = points // own
     point = lax.broadcasted_iota(jnp.int32, (points, LANES), 0)
-    behind = W + 3 * (point % per_row)
+    behind = W + PIECES * (point % per_row)
     packed = jnp.zeros((points, LANES), F32)
-    for k, piece in enumerate(three_pieces(share)):
+    for k, piece in enumerate(in_pieces(share)):
         packed = jnp.where(lane == behind + k, piece, packed)
     fold_row = lax.broadcasted_iota(jnp.int32, (own, points), 0)
     fold_col = lax.broadcasted_iota(jnp.int32, (own, points), 1)
@@ -168,8 +170,8 @@
 
 def final_shares(sizes, place, arrived, block, colloc, shares, rows):
     size_x, _, per_rows = sizes
-    pieces, _, lanes = shares.shape
-    wide = lanes // per_rows
+    pieces, height, lanes = shares.shape
+    wide = height * lanes // (2 * per_rows)
     size_y = pieces // size_x
     part = colloc.shape[1] // size_y
     points = block.shape[0]
@@ -180,11 +182,11 @@
     unfold_col = lax.broadcasted_iota(jnp.int32, (points, own), 1)
     unfold = jnp.where(unfold_row // per_row == unfold_col, 1.0, 0.0).astype(BF16)
     spread_out = jnp.zeros((points, LANES), F32)
-    for piece in three_pieces(total):
+    for piece in in_pieces(total):
         spread_out += times(unfold, piece.astype(BF16))
     lane = lax.broadcasted_iota(jnp.int32, (points, LANES), 1)
-    behind = W + 3 * (lax.broadcasted_iota(jnp.int32, (points, LANES), 0) % per_row)
-    kept = (lane >= behind) & (lane < behind + 3)
+    behind = W + PIECES * (lax.broadcasted_iota(jnp.int32, (points, LANES), 0) % per_row)
+    kept = (lane >= behind) & (lane < behind + PIECES)
     potential = jnp.sum(jnp.where(kept, spread_out, 0.0), axis=1, keepdims=True)
     window = block[:, block.shape[1] - LANES :]
     pick = one_hot((own, LANES), lambda row: row + place[1] * own)
@@ -199,7 +201,12 @@
         return one_hot((size_x * SUBLANES, own), target)
 
     left = times(spread(0), weighted, 1, 1) + times(spread(1), total[:, :points].astype(BF16))
-    rows[:, : colloc.shape[1]] = times(left.astype(BF16), colloc[...])
+    left = left.astype(BF16)
+    width = colloc.shape[1]
+    step = 4 * LANES
+    for at in range(0, width, step):
+        part_of = pl.ds(at, min(step, width - at))
+        rows[:, part_of] = times(left, colloc[:, part_of])
     for c in range(size_y):
         start = c * part // LANES * LANES
         span = wide + LANES
@@ -211,17 +218,23 @@
         for a in range(size_x):
             for b in range(per_rows):
                 at = a * SUBLANES + 2 * b
-                shares[a * size_y + c, :, b * wide : (b + 1) * wide] = found[at : at + 2]
+                for lanes in range(0, wide, LANES):
+                    row, place_in = divmod(b * wide + lanes, shares.shape[2])
+                    shares[a * size_y + c, 2 * row : 2 * row + 2, place_in : place_in + LANES] = found[
+                        at : at + 2, lanes : lanes + LANES
+                    ]
 
 
 def outputs(arrived, coulomb, exchange):
     per_rows, part = coulomb.shape
-    wide = arrived.shape[2] // per_rows
+    _, height, lanes = arrived.shape
+    wide = height * lanes // (2 * per_rows)
     total = jnp.sum(arrived[...].astype(F32), axis=0)
+    joined = jnp.concatenate([total[row : row + 2] for row in range(0, height, 2)], axis=1)
     for b in range(per_rows):
         at = b * wide
-        coulomb[b : b + 1] = total[:1, at : at + part]
-        exchange[b : b + 1] = total[1:, at : at + part]
+        coulomb[b : b + 1] = joined[:1, at : at + part]
+        exchange[b : b + 1] = joined[1:, at : at + part]
 
 
 def work(colloc, occ_coeffs, core):
@@ -285,7 +298,7 @@
         name="after",
     )(cols)
     sent = pl.pallas_call(
-        functools.partial(partial_totals, sizes, 4),
+        functools.partial(partial_totals, sizes, 8),
         in_specs=[IN_SMEM, IN_VMEM, IN_VMEM, IN_VMEM, IN_VMEM, IN_VMEM],
         out_specs=IN_VMEM,
         out_shape=jax.ShapeDtypeStruct((size_x * size_z, own, LANES), BF16),
@@ -299,7 +312,7 @@
         functools.partial(final_shares, sizes),
         in_specs=[IN_SMEM, IN_VMEM, IN_VMEM, IN_VMEM],
         out_specs=IN_VMEM,
-        out_shape=jax.ShapeDtypeStruct((size_x * size_y, 2, per_rows * wide), BF16),
+        out_shape=jax.ShapeDtypeStruct((size_x * size_y, 4, per_rows * wide // 2), BF16),
         scratch_shapes=[pltpu.VMEM((size_x * SUBLANES, (width // LANES + 2) * LANES), F32)],
         compiler_params=PARAMS,
         name="final_shares",

time: 115 us -> 115 us (level)
  no operation moved by 1% of the time
where the time goes in v6:
time: 115 us
  blocking collectives  88.3 us (77%)
  waiting for transfers between devices  10.1 us (9%)
  Pallas kernels  8.64 us (8%)
  starting transfers between devices  6.85 us (6%)
    all_to_all x4, blocking collectives, exchange_pieces(): return lax.all_to_all(pieces, axis, split_axis=0, concat_axis=0, tiled=True)  88.3 us
    all_to_all x1, waiting for transfers between devices, exchange_pieces(): return lax.all_to_all(pieces, axis, split_axis=0, concat_axis=0, tiled=True)  8.4 us
    all_to_all x1, starting transfers between devices, exchange_pieces(): return lax.all_to_all(pieces, axis, split_axis=0, concat_axis=0, tiled=True)  3.45 us
    ppermute x1, starting transfers between devices, work(): far = lax.ppermute(near, 'gy_0', [(0, 1), (1, 0)])  3.39 us
    pallas_call x1, Pallas kernels, work(): pl.pallas_call(functools.partial(occupied, sizes, chunk), in_specs=[IN_SM...  3.11 us
    pallas_call x1, Pallas kernels, work(): pl.pallas_call(functools.partial(partial_totals, sizes, 8), in_specs=[IN_...  2.47 us
  transfers between devices with their start and end apart: 2, of which 2 were waited for; matrix products, arithmetic and copies ran while one was open for 0% of the time, Pallas kernels for 0%

profile of v6, /device:TPU:8, one launch (start us, length us, event | category | flops | bytes accessed | tf_op | source)
XLA Modules:
  0.0 114.6 jit_solution(5627922371355281971)
XLA Ops:
  0.6 0.0 copy-start
  0.6 0.1 pad_add_fusion._.place
  0.7 3.1 %occupied.1 = (bf16[8,96,256]{2,1,0:T(8,128)(2,1)S(1)}, bf16[96,384]{1,0:T(8,128)(2,1)S(1)}, f32[8,8,96]{2,1,0:T(8,128)S(1)}) custom-call(s32[3]{0:T(128)S(1)} %pad_add_fusion._.place, bf16[96,4000]{1,0:T(8,128)(2,1)} %colloc.1, bf16[4000,256]{1,0:T(8,128)(2,1)} %coeffs_hbm.1), custom_call_target="tpu_custom_call" | custom-call | tf_op jit(solution)/shard_map/occupied/pallas_call | solution.py:260
  3.8 0.0 copy-start.2
  3.8 18.1 %all_to_all.25.sums = f32[8,8,96]{2,1,0:T(8,128)S(1)} all-to-all(f32[8,8,96]{2,1,0:T(8,128)S(1)} %get-tuple-element.6), channel_id=1, replica_groups=mesh['gx'=8,'gy_0'=2,'gy_1'=8,'gz'=4] {'gx'}, dimensions={0} | all-to-all | bytes 49152 | tf_op jit(solution)/shard_map/all_to_all | solution.py:26
  22.0 0.0 copy-done
  22.0 0.9 potential_rows.1
  22.9 23.4 %all_to_all.26.near = bf16[8,96,384]{2,1,0:T(8,128)(2,1)S(1)} all-to-all(bf16[8,96,384]{2,1,0:T(8,128)(2,1)S(1)} %potential_rows.1), channel_id=1, replica_groups=mesh['gx'=8,'gy_0'=2,'gy_1'=8,'gz'=4] {'gy_1'}, dimensions={0} | all-to-all | bytes 1179648 | tf_op jit(solution)/shard_map/all_to_all | solution.py:26
  46.2 0.0 copy-done.2
  46.2 3.5 %all-to-all-start = ((bf16[8,96,256]{2,1,0:T(8,128)(2,1)}), bf16[8,96,256]{2,1,0:T(8,128)(2,1)S(1)}, u32[]{:S(2)}, u32[]{:S(2)}) async-start(bf16[8,96,256]{2,1,0:T(8,128)(2,1)} %copy-done.2), calls=%async_computation | async-start | bytes 786432 | tf_op jit(solution)/shard_map/all_to_all | solution.py:26
  49.7 3.4 %collective-permute-start = (bf16[8,96,384]{2,1,0:T(8,128)(2,1)S(1)}, bf16[8,96,384]{2,1,0:T(8,128)(2,1)}, u32[]{:S(2)}, u32[]{:S(2)}) collective-permute-start(bf16[8,96,384]{2,1,0:T(8,128)(2,1)S(1)} %all_to_all.26.near), channel_id=1, source_target_pairs={{0,32},{32,0},{1,33},{33,1},{2,34},{34,2},{3,35},{35,3},{4,36},{36... | collective-permute-start | bytes 1769480 | tf_op jit(solution)/shard_map/ppermute | solution.py:289
  53.1 8.4 %all-to-all-done.cols = bf16[8,96,256]{2,1,0:T(8,128)(2,1)S(1)} async-done(((bf16[8,96,256]{2,1,0:T(8,128)(2,1)}), bf16[8,96,256]{2,1,0:T(8,128)(2,1)S(1)}, u32[]{:S(2)}, u32[]{:S(2)}) %all-to-all-start) | async-done | bytes 393248 | tf_op jit(solution)/shard_map/all_to_all | solution.py:26
  61.5 0.0 copy-start.1
  61.5 1.7 %collective-permute-done.far = bf16[8,96,384]{2,1,0:T(8,128)(2,1)} collective-permute-done((bf16[8,96,384]{2,1,0:T(8,128)(2,1)S(1)}, bf16[8,96,384]{2,1,0:T(8,128)(2,1)}, u32[]{:S(2)}, u32[]{:S(2)}) %collective-permute-start) | collective-permute-done | bytes 589856 | tf_op jit(solution)/shard_map/ppermute | solution.py:289
  63.2 2.5 %partial_totals.1 = bf16[32,24,128]{2,1,0:T(8,128)(2,1)S(1)} custom-call(s32[3]{0:T(128)S(1)} %pad_add_fusion._.place, f32[8,128]{1,0:T(8,128)S(1)} %after.1._, bf16[8,96,384]{2,1,0:T(8,128)(2,1)S(1)} %all_to_all.26.near, bf16[8,96,384]{2,1,0:T(8,128)(2,1)} %collective-permute-done.far, bf16[8,96,256]{2,1,0:T(8,128)(2,1)S(1)} %all-to-all-done.cols, ...), custom_call_target="tpu_custom_call" | custom-call | tf_op jit(solution)/shard_map/partial_totals/pallas_call | solution.py:300
  65.6 21.3 %all_to_all.27.arrived = bf16[32,24,128]{2,1,0:T(8,128)(2,1)S(1)} all-to-all(bf16[32,24,128]{2,1,0:T(8,128)(2,1)S(1)} %partial_totals.1), channel_id=1, replica_groups=mesh['gx'=8,'gy_0'=2,'gy_1'=8,'gz'=4] {'gx','gz'}, dimensions={0} | all-to-all | bytes 393216 | tf_op jit(solution)/shard_map/all_to_all | solution.py:26
  86.9 0.0 copy-done.1
  86.9 1.4 %final_shares.1 = bf16[128,4,384]{2,1,0:T(4,128)(2,1)S(1)} custom-call(s32[3]{0:T(128)S(1)} %pad_add_fusion._.place, bf16[32,24,128]{2,1,0:T(8,128)(2,1)S(1)} %all_to_all.27.arrived, bf16[96,384]{1,0:T(8,128)(2,1)S(1)} %get-tuple-element.7.block, bf16[96,4000]{1,0:T(8,128)(2,1)S(1)} %copy-done.1), custom_call_target="tpu_custom_call" | custom-call | tf_op jit(solution)/shard_map/final_shares/pallas_call | solution.py:311
  88.4 25.5 %all_to_all.28.arrived = bf16[128,4,384]{2,1,0:T(4,128)(2,1)S(1)} all-to-all(bf16[128,4,384]{2,1,0:T(4,128)(2,1)S(1)} %final_shares.1), channel_id=1, replica_groups=mesh['gx'=8,'gy_0'=2,'gy_1'=8,'gz'=4] {'gx','gy_0','gy_1'}, dimensions={0} | all-to-all | bytes 786432 | tf_op jit(solution)/shard_map/all_to_all | solution.py:26
  113.8 0.8 outputs.1
  (1 shorter events, 0.0 us)
Async XLA Ops:
  0.6 21.4 %copy-start = (bf16[1536,1,768]{2,0,1:T(8,128)(2,1)S(1)}, bf16[1536,1,768]{2,0,1:T(8,128)(2,1)}, u32[]{:S(2)}) copy-start(bf16[1536,1,768]{2,0,1:T(8,128)(2,1)} %param.5) | copy-start | bytes 7077892
  3.8 42.4 %copy-start.2 = (bf16[8,96,256]{2,1,0:T(8,128)(2,1)}, bf16[8,96,256]{2,1,0:T(8,128)(2,1)S(1)}, u32[]{:S(2)}) copy-start(bf16[8,96,256]{2,1,0:T(8,128)(2,1)S(1)} %get-tuple-element.5) | copy-start | bytes 1179652
  46.2 15.3 %all-to-all-start = ((bf16[8,96,256]{2,1,0:T(8,128)(2,1)}), bf16[8,96,256]{2,1,0:T(8,128)(2,1)S(1)}, u32[]{:S(2)}, u32[]{:S(2)}) async-start(bf16[8,96,256]{2,1,0:T(8,128)(2,1)} %copy-done.2), calls=%async_computation | async-start | bytes 786432 | tf_op jit(solution)/shard_map/all_to_all | solution.py:26
  49.7 13.5 %collective-permute-start = (bf16[8,96,384]{2,1,0:T(8,128)(2,1)S(1)}, bf16[8,96,384]{2,1,0:T(8,128)(2,1)}, u32[]{:S(2)}, u32[]{:S(2)}) collective-permute-start(bf16[8,96,384]{2,1,0:T(8,128)(2,1)S(1)} %all_to_all.26.near), channel_id=1, source_target_pairs={{0,32},{32,0},{1,33},{33,1},{2,34},{34,2},{3,35},{35,3},{4,36},{36... | collective-permute-start | bytes 1769480 | tf_op jit(solution)/shard_map/ppermute | solution.py:289
  61.5 25.5 %copy-start.1 = (bf16[96,4000]{1,0:T(8,128)(2,1)S(1)}, bf16[96,4000]{1,0:T(8,128)(2,1)}, u32[]{:S(2)}) copy-start(bf16[96,4000]{1,0:T(8,128)(2,1)} %colloc.1) | copy-start | bytes 2304004

commit v7 on v6

--- a/solution.py
+++ b/solution.py
@@ -68,7 +68,7 @@
         return ((col % own) // per_rows) * (size_z * per_rows) + (col // own) * per_rows + col % per_rows
 
     pick = one_hot((LANES, LANES), lambda rows: jnp.where(rows < W, source(rows), -1))
-    square = one_hot((points, points), lambda rows: rows)
+    square = one_hot((points, LANES), lambda rows: rows)
     acc = jnp.zeros((points, group), F32)
     for (first, second), at in zip(copies_in, starts):
         first.wait()
@@ -80,7 +80,7 @@
     occ = acc.astype(BF16)
     vals = occ.astype(F32)
     density = jnp.sum(vals * vals, axis=1, keepdims=True).astype(BF16)
-    density = times(jnp.broadcast_to(density, (points, LANES)), square, 0, 0)[: sums.shape[1]]
+    density = times(jnp.broadcast_to(density, (points, LANES)), square, 0, 0)[: sums.shape[1]].astype(BF16)
     block[:, :group] = occ
     for a in range(size_x):
         sums[a] = density
@@ -88,11 +88,11 @@
 
 
 def potential_rows(sums, block, core, copies, density, shares):
-    size_x, _, points = sums.shape
-    size_y = copies.shape[0]
+    size_x = sums.shape[0]
+    size_y, points, _ = copies.shape
     group = block.shape[1] - LANES
     for a in range(size_x):
-        density[:, a * points : (a + 1) * points] = sums[a]
+        density[:2, a * points : (a + 1) * points] = sums[a].astype(F32)[:, :points]
     right = jnp.broadcast_to(density[:1, :], (LANES, size_x * points)).astype(BF16)
     lane = lax.broadcasted_iota(jnp.int32, (points, LANES), 1)
     occ = block[:, :group]
@@ -264,7 +264,7 @@
         out_shape=[
             jax.ShapeDtypeStruct((size_x, points, group), BF16),
             jax.ShapeDtypeStruct((points, group + LANES), BF16),
-            jax.ShapeDtypeStruct((size_x, 8, points), F32),
+            jax.ShapeDtypeStruct((size_x, 2, LANES), BF16),
         ],
         scratch_shapes=[
             pltpu.VMEM((points, width), BF16),

time: 115 us -> 115 us (level)
  no operation moved by 1% of the time
where the time goes in v7:
time: 115 us; the launch traced here: 114 us
  blocking collectives  88 us (77%)
  waiting for transfers between devices  10.1 us (9%)
  Pallas kernels  8.63 us (8%)
  starting transfers between devices  6.85 us (6%)
    all_to_all x4, blocking collectives, exchange_pieces(): return lax.all_to_all(pieces, axis, split_axis=0, concat_axis=0, tiled=True)  88 us
    all_to_all x1, waiting for transfers between devices, exchange_pieces(): return lax.all_to_all(pieces, axis, split_axis=0, concat_axis=0, tiled=True)  8.4 us
    all_to_all x1, starting transfers between devices, exchange_pieces(): return lax.all_to_all(pieces, axis, split_axis=0, concat_axis=0, tiled=True)  3.45 us
    ppermute x1, starting transfers between devices, work(): far = lax.ppermute(near, 'gy_0', [(0, 1), (1, 0)])  3.39 us
    pallas_call x1, Pallas kernels, work(): pl.pallas_call(functools.partial(occupied, sizes, chunk), in_specs=[IN_SM...  3.11 us
    pallas_call x1, Pallas kernels, work(): pl.pallas_call(functools.partial(partial_totals, sizes, 8), in_specs=[IN_...  2.46 us
  transfers between devices with their start and end apart: 2, of which 2 were waited for; matrix products, arithmetic and copies ran while one was open for 0% of the time, Pallas kernels for 0%

profile of v7, /device:TPU:8, one launch (start us, length us, event | category | flops | bytes accessed | tf_op | source)
XLA Modules:
  0.0 114.3 jit_solution(6079087137382346167)
XLA Ops:
  0.6 0.0 copy-start
  0.6 0.1 pad_add_fusion._.place
  0.7 3.1 %occupied.1 = (bf16[8,96,256]{2,1,0:T(8,128)(2,1)S(1)}, bf16[96,384]{1,0:T(8,128)(2,1)S(1)}, bf16[8,2,128]{2,1,0:T(2,128)(2,1)S(1)}) custom-call(s32[3]{0:T(128)S(1)} %pad_add_fusion._.place, bf16[96,4000]{1,0:T(8,128)(2,1)} %colloc.1, bf16[4000,256]{1,0:T(8,128)(2,1)} %coeffs_hbm.1), custom_call_target="tpu_custom_call" | custom-call | tf_op jit(solution)/shard_map/occupied/pallas_call | solution.py:260
  3.8 0.0 copy-start.2
  3.8 17.8 %all_to_all.25.sums = bf16[8,2,128]{2,1,0:T(2,128)(2,1)S(1)} all-to-all(bf16[8,2,128]{2,1,0:T(2,128)(2,1)S(1)} %get-tuple-element.6), channel_id=1, replica_groups=mesh['gx'=8,'gy_0'=2,'gy_1'=8,'gz'=4] {'gx'}, dimensions={0} | all-to-all | bytes 8192 | tf_op jit(solution)/shard_map/all_to_all | solution.py:26
  21.7 0.0 copy-done
  21.7 0.9 potential_rows.1
  22.5 23.4 %all_to_all.26.near = bf16[8,96,384]{2,1,0:T(8,128)(2,1)S(1)} all-to-all(bf16[8,96,384]{2,1,0:T(8,128)(2,1)S(1)} %potential_rows.1), channel_id=1, replica_groups=mesh['gx'=8,'gy_0'=2,'gy_1'=8,'gz'=4] {'gy_1'}, dimensions={0} | all-to-all | bytes 1179648 | tf_op jit(solution)/shard_map/all_to_all | solution.py:26
  45.9 0.0 copy-done.2
  45.9 3.5 %all-to-all-start = ((bf16[8,96,256]{2,1,0:T(8,128)(2,1)}), bf16[8,96,256]{2,1,0:T(8,128)(2,1)S(1)}, u32[]{:S(2)}, u32[]{:S(2)}) async-start(bf16[8,96,256]{2,1,0:T(8,128)(2,1)} %copy-done.2), calls=%async_computation | async-start | bytes 786432 | tf_op jit(solution)/shard_map/all_to_all | solution.py:26
  49.4 3.4 %collective-permute-start = (bf16[8,96,384]{2,1,0:T(8,128)(2,1)S(1)}, bf16[8,96,384]{2,1,0:T(8,128)(2,1)}, u32[]{:S(2)}, u32[]{:S(2)}) collective-permute-start(bf16[8,96,384]{2,1,0:T(8,128)(2,1)S(1)} %all_to_all.26.near), channel_id=1, source_target_pairs={{0,32},{32,0},{1,33},{33,1},{2,34},{34,2},{3,35},{35,3},{4,36},{36... | collective-permute-start | bytes 1769480 | tf_op jit(solution)/shard_map/ppermute | solution.py:289
  52.8 8.4 %all-to-all-done.cols = bf16[8,96,256]{2,1,0:T(8,128)(2,1)S(1)} async-done(((bf16[8,96,256]{2,1,0:T(8,128)(2,1)}), bf16[8,96,256]{2,1,0:T(8,128)(2,1)S(1)}, u32[]{:S(2)}, u32[]{:S(2)}) %all-to-all-start) | async-done | bytes 393248 | tf_op jit(solution)/shard_map/all_to_all | solution.py:26
  61.2 0.0 copy-start.1
  61.2 1.7 %collective-permute-done.far = bf16[8,96,384]{2,1,0:T(8,128)(2,1)} collective-permute-done((bf16[8,96,384]{2,1,0:T(8,128)(2,1)S(1)}, bf16[8,96,384]{2,1,0:T(8,128)(2,1)}, u32[]{:S(2)}, u32[]{:S(2)}) %collective-permute-start) | collective-permute-done | bytes 589856 | tf_op jit(solution)/shard_map/ppermute | solution.py:289
  62.8 2.5 %partial_totals.1 = bf16[32,24,128]{2,1,0:T(8,128)(2,1)S(1)} custom-call(s32[3]{0:T(128)S(1)} %pad_add_fusion._.place, f32[8,128]{1,0:T(8,128)S(1)} %after.1._, bf16[8,96,384]{2,1,0:T(8,128)(2,1)S(1)} %all_to_all.26.near, bf16[8,96,384]{2,1,0:T(8,128)(2,1)} %collective-permute-done.far, bf16[8,96,256]{2,1,0:T(8,128)(2,1)S(1)} %all-to-all-done.cols, ...), custom_call_target="tpu_custom_call" | custom-call | tf_op jit(solution)/shard_map/partial_totals/pallas_call | solution.py:300
  65.3 21.3 %all_to_all.27.arrived = bf16[32,24,128]{2,1,0:T(8,128)(2,1)S(1)} all-to-all(bf16[32,24,128]{2,1,0:T(8,128)(2,1)S(1)} %partial_totals.1), channel_id=1, replica_groups=mesh['gx'=8,'gy_0'=2,'gy_1'=8,'gz'=4] {'gx','gz'}, dimensions={0} | all-to-all | bytes 393216 | tf_op jit(solution)/shard_map/all_to_all | solution.py:26
  86.6 0.0 copy-done.1
  86.6 1.4 %final_shares.1 = bf16[128,4,384]{2,1,0:T(4,128)(2,1)S(1)} custom-call(s32[3]{0:T(128)S(1)} %pad_add_fusion._.place, bf16[32,24,128]{2,1,0:T(8,128)(2,1)S(1)} %all_to_all.27.arrived, bf16[96,384]{1,0:T(8,128)(2,1)S(1)} %get-tuple-element.7.block, bf16[96,4000]{1,0:T(8,128)(2,1)S(1)} %copy-done.1), custom_call_target="tpu_custom_call" | custom-call | tf_op jit(solution)/shard_map/final_shares/pallas_call | solution.py:311
  88.1 25.5 %all_to_all.28.arrived = bf16[128,4,384]{2,1,0:T(4,128)(2,1)S(1)} all-to-all(bf16[128,4,384]{2,1,0:T(4,128)(2,1)S(1)} %final_shares.1), channel_id=1, replica_groups=mesh['gx'=8,'gy_0'=2,'gy_1'=8,'gz'=4] {'gx','gy_0','gy_1'}, dimensions={0} | all-to-all | bytes 786432 | tf_op jit(solution)/shard_map/all_to_all | solution.py:26
  113.5 0.8 outputs.1
  (1 shorter events, 0.0 us)
Async XLA Ops:
  0.6 21.0 %copy-start = (bf16[1536,1,768]{2,0,1:T(8,128)(2,1)S(1)}, bf16[1536,1,768]{2,0,1:T(8,128)(2,1)}, u32[]{:S(2)}) copy-start(bf16[1536,1,768]{2,0,1:T(8,128)(2,1)} %param.5) | copy-start | bytes 7077892
  3.8 42.1 %copy-start.2 = (bf16[8,96,256]{2,1,0:T(8,128)(2,1)}, bf16[8,96,256]{2,1,0:T(8,128)(2,1)S(1)}, u32[]{:S(2)}) copy-start(bf16[8,96,256]{2,1,0:T(8,128)(2,1)S(1)} %get-tuple-element.5) | copy-start | bytes 1179652
  45.9 15.3 %all-to-all-start = ((bf16[8,96,256]{2,1,0:T(8,128)(2,1)}), bf16[8,96,256]{2,1,0:T(8,128)(2,1)S(1)}, u32[]{:S(2)}, u32[]{:S(2)}) async-start(bf16[8,96,256]{2,1,0:T(8,128)(2,1)} %copy-done.2), calls=%async_computation | async-start | bytes 786432 | tf_op jit(solution)/shard_map/all_to_all | solution.py:26
  49.4 13.5 %collective-permute-start = (bf16[8,96,384]{2,1,0:T(8,128)(2,1)S(1)}, bf16[8,96,384]{2,1,0:T(8,128)(2,1)}, u32[]{:S(2)}, u32[]{:S(2)}) collective-permute-start(bf16[8,96,384]{2,1,0:T(8,128)(2,1)S(1)} %all_to_all.26.near), channel_id=1, source_target_pairs={{0,32},{32,0},{1,33},{33,1},{2,34},{34,2},{3,35},{35,3},{4,36},{36... | collective-permute-start | bytes 1769480 | tf_op jit(solution)/shard_map/ppermute | solution.py:289
  61.2 25.5 %copy-start.1 = (bf16[96,4000]{1,0:T(8,128)(2,1)S(1)}, bf16[96,4000]{1,0:T(8,128)(2,1)}, u32[]{:S(2)}) copy-start(bf16[96,4000]{1,0:T(8,128)(2,1)} %colloc.1) | copy-start | bytes 2304004

commit v8 on v7

--- a/solution.py
+++ b/solution.py
@@ -49,10 +49,11 @@
     size_x, size_z, per_rows = sizes
     width, group = coeffs.shape
     points = colloc.shape[0]
-    starts = range(0, width, chunk)
+    starts = [0, chunk, 2 * chunk, width // LANES * LANES - 3 * LANES]
+    widths = [after_it - at for at, after_it in zip(starts, starts[1:] + [width])]
     copies_in = []
-    for k, at in enumerate(starts):
-        part = pl.ds(at, min(chunk, width - at))
+    for k, (at, size) in enumerate(zip(starts, widths)):
+        part = pl.ds(at, size)
         copies_in.append(
             (
                 pltpu.make_async_copy(colloc_hbm.at[:, part], colloc.at[:, part], sems.at[0, k]),
@@ -70,10 +71,10 @@
     pick = one_hot((LANES, LANES), lambda rows: jnp.where(rows < W, source(rows), -1))
     square = one_hot((points, LANES), lambda rows: rows)
     acc = jnp.zeros((points, group), F32)
-    for (first, second), at in zip(copies_in, starts):
+    for (first, second), at, size in zip(copies_in, starts, widths):
         first.wait()
         second.wait()
-        part = pl.ds(at, min(chunk, width - at))
+        part = pl.ds(at, size)
         acc += times(colloc[:, part], coeffs[part, :])
         if at == 0:
             block[:, group:] = times(colloc[:, :LANES], pick, 1, 1).astype(BF16)
@@ -216,25 +217,22 @@
             found = pltpu.roll(found, span - shift, 1)
         found = found[:, :wide].astype(BF16)
         for a in range(size_x):
-            for b in range(per_rows):
-                at = a * SUBLANES + 2 * b
-                for lanes in range(0, wide, LANES):
-                    row, place_in = divmod(b * wide + lanes, shares.shape[2])
-                    shares[a * size_y + c, 2 * row : 2 * row + 2, place_in : place_in + LANES] = found[
-                        at : at + 2, lanes : lanes + LANES
-                    ]
+            at = a * SUBLANES
+            shares[a * size_y + c, :, :wide] = found[at : at + 4]
+            for k in range(2):
+                shares[a * size_y + c, 2 * k : 2 * k + 2, wide:] = found[
+                    at + 4 : at + 6, k * LANES : (k + 1) * LANES
+                ]
 
 
 def outputs(arrived, coulomb, exchange):
-    per_rows, part = coulomb.shape
-    _, height, lanes = arrived.shape
-    wide = height * lanes // (2 * per_rows)
+    part = coulomb.shape[1]
+    wide = arrived.shape[2] - LANES
     total = jnp.sum(arrived[...].astype(F32), axis=0)
-    joined = jnp.concatenate([total[row : row + 2] for row in range(0, height, 2)], axis=1)
-    for b in range(per_rows):
-        at = b * wide
-        coulomb[b : b + 1] = joined[:1, at : at + part]
-        exchange[b : b + 1] = joined[1:, at : at + part]
+    last = jnp.concatenate([total[:2, wide:], total[2:, wide:]], axis=1)
+    for b, pair in enumerate((total[:2], total[2:], last)):
+        coulomb[b : b + 1] = pair[:1, :part]
+        exchange[b : b + 1] = pair[1:, :part]
 
 
 def work(colloc, occ_coeffs, core):
@@ -254,8 +252,8 @@
     core_flat = core.reshape(row_count, flat_cols)
     place = jnp.stack([lax.axis_index("gx"), lax.axis_index("gz"), lax.axis_index("gy_0")])
     place = place.astype(jnp.int32)
-    chunk = 8 * LANES
-    steps = -(-width // chunk)
+    chunk = 10 * LANES
+    steps = 4
 
     copies, block, sums = pl.pallas_call(
         functools.partial(occupied, sizes, chunk),

time: 115 us -> 115 us (level)
  no operation moved by 1% of the time
where the time goes in v8:
time: 115 us; the launch traced here: 114 us
  blocking collectives  88 us (77%)
  waiting for transfers between devices  10.1 us (9%)
  Pallas kernels  8.67 us (8%)
  starting transfers between devices  6.85 us (6%)
    all_to_all x4, blocking collectives, exchange_pieces(): return lax.all_to_all(pieces, axis, split_axis=0, concat_axis=0, tiled=True)  88 us
    all_to_all x1, waiting for transfers between devices, exchange_pieces(): return lax.all_to_all(pieces, axis, split_axis=0, concat_axis=0, tiled=True)  8.4 us
    all_to_all x1, starting transfers between devices, exchange_pieces(): return lax.all_to_all(pieces, axis, split_axis=0, concat_axis=0, tiled=True)  3.45 us
    ppermute x1, starting transfers between devices, work(): far = lax.ppermute(near, 'gy_0', [(0, 1), (1, 0)])  3.39 us
    pallas_call x1, Pallas kernels, work(): pl.pallas_call(functools.partial(occupied, sizes, chunk), in_specs=[IN_SM...  3.18 us
    pallas_call x1, Pallas kernels, work(): pl.pallas_call(functools.partial(partial_totals, sizes, 8), in_specs=[IN_...  2.46 us
  transfers between devices with their start and end apart: 2, of which 2 were waited for; matrix products, arithmetic and copies ran while one was open for 0% of the time, Pallas kernels for 0%

profile of v8, /device:TPU:8, one launch (start us, length us, event | category | flops | bytes accessed | tf_op | source)
XLA Modules:
  0.0 114.4 jit_solution(10520543482232986640)
XLA Ops:
  0.6 0.0 copy-start
  0.6 0.1 pad_add_fusion._.place
  0.7 3.2 %occupied.1 = (bf16[8,96,256]{2,1,0:T(8,128)(2,1)S(1)}, bf16[96,384]{1,0:T(8,128)(2,1)S(1)}, bf16[8,2,128]{2,1,0:T(2,128)(2,1)S(1)}) custom-call(s32[3]{0:T(128)S(1)} %pad_add_fusion._.place, bf16[96,4000]{1,0:T(8,128)(2,1)} %colloc.1, bf16[4000,256]{1,0:T(8,128)(2,1)} %coeffs_hbm.1), custom_call_target="tpu_custom_call" | custom-call | tf_op jit(solution)/shard_map/occupied/pallas_call | solution.py:258
  3.9 0.0 copy-start.2
  3.9 17.8 %all_to_all.25.sums = bf16[8,2,128]{2,1,0:T(2,128)(2,1)S(1)} all-to-all(bf16[8,2,128]{2,1,0:T(2,128)(2,1)S(1)} %get-tuple-element.6), channel_id=1, replica_groups=mesh['gx'=8,'gy_0'=2,'gy_1'=8,'gz'=4] {'gx'}, dimensions={0} | all-to-all | bytes 8192 | tf_op jit(solution)/shard_map/all_to_all | solution.py:26
  21.7 0.0 copy-done
  21.7 0.9 potential_rows.1
  22.6 23.4 %all_to_all.26.near = bf16[8,96,384]{2,1,0:T(8,128)(2,1)S(1)} all-to-all(bf16[8,96,384]{2,1,0:T(8,128)(2,1)S(1)} %potential_rows.1), channel_id=1, replica_groups=mesh['gx'=8,'gy_0'=2,'gy_1'=8,'gz'=4] {'gy_1'}, dimensions={0} | all-to-all | bytes 1179648 | tf_op jit(solution)/shard_map/all_to_all | solution.py:26
  46.0 0.0 copy-done.2
  46.0 3.5 %all-to-all-start = ((bf16[8,96,256]{2,1,0:T(8,128)(2,1)}), bf16[8,96,256]{2,1,0:T(8,128)(2,1)S(1)}, u32[]{:S(2)}, u32[]{:S(2)}) async-start(bf16[8,96,256]{2,1,0:T(8,128)(2,1)} %copy-done.2), calls=%async_computation | async-start | bytes 786432 | tf_op jit(solution)/shard_map/all_to_all | solution.py:26
  49.4 3.4 %collective-permute-start = (bf16[8,96,384]{2,1,0:T(8,128)(2,1)S(1)}, bf16[8,96,384]{2,1,0:T(8,128)(2,1)}, u32[]{:S(2)}, u32[]{:S(2)}) collective-permute-start(bf16[8,96,384]{2,1,0:T(8,128)(2,1)S(1)} %all_to_all.26.near), channel_id=1, source_target_pairs={{0,32},{32,0},{1,33},{33,1},{2,34},{34,2},{3,35},{35,3},{4,36},{36... | collective-permute-start | bytes 1769480 | tf_op jit(solution)/shard_map/ppermute | solution.py:287
  52.8 8.4 %all-to-all-done.cols = bf16[8,96,256]{2,1,0:T(8,128)(2,1)S(1)} async-done(((bf16[8,96,256]{2,1,0:T(8,128)(2,1)}), bf16[8,96,256]{2,1,0:T(8,128)(2,1)S(1)}, u32[]{:S(2)}, u32[]{:S(2)}) %all-to-all-start) | async-done | bytes 393248 | tf_op jit(solution)/shard_map/all_to_all | solution.py:26
  61.2 0.0 copy-start.1
  61.2 1.7 %collective-permute-done.far = bf16[8,96,384]{2,1,0:T(8,128)(2,1)} collective-permute-done((bf16[8,96,384]{2,1,0:T(8,128)(2,1)S(1)}, bf16[8,96,384]{2,1,0:T(8,128)(2,1)}, u32[]{:S(2)}, u32[]{:S(2)}) %collective-permute-start) | collective-permute-done | bytes 589856 | tf_op jit(solution)/shard_map/ppermute | solution.py:287
  62.9 2.5 %partial_totals.1 = bf16[32,24,128]{2,1,0:T(8,128)(2,1)S(1)} custom-call(s32[3]{0:T(128)S(1)} %pad_add_fusion._.place, f32[8,128]{1,0:T(8,128)S(1)} %after.1._, bf16[8,96,384]{2,1,0:T(8,128)(2,1)S(1)} %all_to_all.26.near, bf16[8,96,384]{2,1,0:T(8,128)(2,1)} %collective-permute-done.far, bf16[8,96,256]{2,1,0:T(8,128)(2,1)S(1)} %all-to-all-done.cols, ...), custom_call_target="tpu_custom_call" | custom-call | tf_op jit(solution)/shard_map/partial_totals/pallas_call | solution.py:298
  65.4 21.3 %all_to_all.27.arrived = bf16[32,24,128]{2,1,0:T(8,128)(2,1)S(1)} all-to-all(bf16[32,24,128]{2,1,0:T(8,128)(2,1)S(1)} %partial_totals.1), channel_id=1, replica_groups=mesh['gx'=8,'gy_0'=2,'gy_1'=8,'gz'=4] {'gx','gz'}, dimensions={0} | all-to-all | bytes 393216 | tf_op jit(solution)/shard_map/all_to_all | solution.py:26
  86.7 0.0 copy-done.1
  86.7 1.4 %final_shares.1 = bf16[128,4,384]{2,1,0:T(4,128)(2,1)S(1)} custom-call(s32[3]{0:T(128)S(1)} %pad_add_fusion._.place, bf16[32,24,128]{2,1,0:T(8,128)(2,1)S(1)} %all_to_all.27.arrived, bf16[96,384]{1,0:T(8,128)(2,1)S(1)} %get-tuple-element.7.block, bf16[96,4000]{1,0:T(8,128)(2,1)S(1)} %copy-done.1), custom_call_target="tpu_custom_call" | custom-call | tf_op jit(solution)/shard_map/final_shares/pallas_call | solution.py:309
  88.1 25.5 %all_to_all.28.arrived = bf16[128,4,384]{2,1,0:T(4,128)(2,1)S(1)} all-to-all(bf16[128,4,384]{2,1,0:T(4,128)(2,1)S(1)} %final_shares.1), channel_id=1, replica_groups=mesh['gx'=8,'gy_0'=2,'gy_1'=8,'gz'=4] {'gx','gy_0','gy_1'}, dimensions={0} | all-to-all | bytes 786432 | tf_op jit(solution)/shard_map/all_to_all | solution.py:26
  113.6 0.8 outputs.1
  (1 shorter events, 0.0 us)
Async XLA Ops:
  0.6 21.1 %copy-start = (bf16[1536,1,768]{2,0,1:T(8,128)(2,1)S(1)}, bf16[1536,1,768]{2,0,1:T(8,128)(2,1)}, u32[]{:S(2)}) copy-start(bf16[1536,1,768]{2,0,1:T(8,128)(2,1)} %param.5) | copy-start | bytes 7077892
  3.9 42.1 %copy-start.2 = (bf16[8,96,256]{2,1,0:T(8,128)(2,1)}, bf16[8,96,256]{2,1,0:T(8,128)(2,1)S(1)}, u32[]{:S(2)}) copy-start(bf16[8,96,256]{2,1,0:T(8,128)(2,1)S(1)} %get-tuple-element.5) | copy-start | bytes 1179652
  46.0 15.3 %all-to-all-start = ((bf16[8,96,256]{2,1,0:T(8,128)(2,1)}), bf16[8,96,256]{2,1,0:T(8,128)(2,1)S(1)}, u32[]{:S(2)}, u32[]{:S(2)}) async-start(bf16[8,96,256]{2,1,0:T(8,128)(2,1)} %copy-done.2), calls=%async_computation | async-start | bytes 786432 | tf_op jit(solution)/shard_map/all_to_all | solution.py:26
  49.4 13.5 %collective-permute-start = (bf16[8,96,384]{2,1,0:T(8,128)(2,1)S(1)}, bf16[8,96,384]{2,1,0:T(8,128)(2,1)}, u32[]{:S(2)}, u32[]{:S(2)}) collective-permute-start(bf16[8,96,384]{2,1,0:T(8,128)(2,1)S(1)} %all_to_all.26.near), channel_id=1, source_target_pairs={{0,32},{32,0},{1,33},{33,1},{2,34},{34,2},{3,35},{35,3},{4,36},{36... | collective-permute-start | bytes 1769480 | tf_op jit(solution)/shard_map/ppermute | solution.py:287
  61.2 25.5 %copy-start.1 = (bf16[96,4000]{1,0:T(8,128)(2,1)S(1)}, bf16[96,4000]{1,0:T(8,128)(2,1)}, u32[]{:S(2)}) copy-start(bf16[96,4000]{1,0:T(8,128)(2,1)} %colloc.1) | copy-start | bytes 2304004

commit v9 on v8

--- a/solution.py
+++ b/solution.py
@@ -69,7 +69,6 @@
         return ((col % own) // per_rows) * (size_z * per_rows) + (col // own) * per_rows + col % per_rows
 
     pick = one_hot((LANES, LANES), lambda rows: jnp.where(rows < W, source(rows), -1))
-    square = one_hot((points, LANES), lambda rows: rows)
     acc = jnp.zeros((points, group), F32)
     for (first, second), at, size in zip(copies_in, starts, widths):
         first.wait()
@@ -80,11 +79,12 @@
             block[:, group:] = times(colloc[:, :LANES], pick, 1, 1).astype(BF16)
     occ = acc.astype(BF16)
     vals = occ.astype(F32)
-    density = jnp.sum(vals * vals, axis=1, keepdims=True).astype(BF16)
-    density = times(jnp.broadcast_to(density, (points, LANES)), square, 0, 0)[: sums.shape[1]].astype(BF16)
+    ones = jnp.ones((SUBLANES, group), BF16)
+    density = sum(times(ones, piece.astype(BF16), 1, 1) for piece in in_pieces(vals * vals))
+    density = density[: sums.shape[1]].astype(BF16)
     block[:, :group] = occ
     for a in range(size_x):
-        sums[a] = density
+        sums[a, :, :points] = density
         copies[a] = occ
 
 

time: 115 us -> 115 us (level)
  no operation moved by 1% of the time
where the time goes in v9:
time: 115 us; the launch traced here: 114 us
  blocking collectives  88 us (77%)
  waiting for transfers between devices  10.1 us (9%)
  Pallas kernels  8.57 us (7%)
  starting transfers between devices  6.86 us (6%)
    all_to_all x4, blocking collectives, exchange_pieces(): return lax.all_to_all(pieces, axis, split_axis=0, concat_axis=0, tiled=True)  88 us
    all_to_all x1, waiting for transfers between devices, exchange_pieces(): return lax.all_to_all(pieces, axis, split_axis=0, concat_axis=0, tiled=True)  8.38 us
    all_to_all x1, starting transfers between devices, exchange_pieces(): return lax.all_to_all(pieces, axis, split_axis=0, concat_axis=0, tiled=True)  3.45 us
    ppermute x1, starting transfers between devices, work(): far = lax.ppermute(near, 'gy_0', [(0, 1), (1, 0)])  3.41 us
    pallas_call x1, Pallas kernels, work(): pl.pallas_call(functools.partial(occupied, sizes, chunk), in_specs=[IN_SM...  3.08 us
    pallas_call x1, Pallas kernels, work(): pl.pallas_call(functools.partial(partial_totals, sizes, 8), in_specs=[IN_...  2.46 us
  transfers between devices with their start and end apart: 2, of which 2 were waited for; matrix products, arithmetic and copies ran while one was open for 0% of the time, Pallas kernels for 0%

profile of v9, /device:TPU:8, one launch (start us, length us, event | category | flops | bytes accessed | tf_op | source)
XLA Modules:
  0.0 114.3 jit_solution(7255236040688044251)
XLA Ops:
  0.6 0.0 copy-start
  0.6 0.1 pad_add_fusion._.place
  0.7 3.1 %occupied.1 = (bf16[8,96,256]{2,1,0:T(8,128)(2,1)S(1)}, bf16[96,384]{1,0:T(8,128)(2,1)S(1)}, bf16[8,2,128]{2,1,0:T(2,128)(2,1)S(1)}) custom-call(s32[3]{0:T(128)S(1)} %pad_add_fusion._.place, bf16[96,4000]{1,0:T(8,128)(2,1)} %colloc.1, bf16[4000,256]{1,0:T(8,128)(2,1)} %coeffs_hbm.1), custom_call_target="tpu_custom_call" | custom-call | tf_op jit(solution)/shard_map/occupied/pallas_call | solution.py:258
  3.8 0.0 copy-start.2
  3.8 17.8 %all_to_all.25.sums = bf16[8,2,128]{2,1,0:T(2,128)(2,1)S(1)} all-to-all(bf16[8,2,128]{2,1,0:T(2,128)(2,1)S(1)} %get-tuple-element.6), channel_id=1, replica_groups=mesh['gx'=8,'gy_0'=2,'gy_1'=8,'gz'=4] {'gx'}, dimensions={0} | all-to-all | bytes 8192 | tf_op jit(solution)/shard_map/all_to_all | solution.py:26
  21.6 0.0 copy-done
  21.6 0.9 potential_rows.1
  22.5 23.4 %all_to_all.26.near = bf16[8,96,384]{2,1,0:T(8,128)(2,1)S(1)} all-to-all(bf16[8,96,384]{2,1,0:T(8,128)(2,1)S(1)} %potential_rows.1), channel_id=1, replica_groups=mesh['gx'=8,'gy_0'=2,'gy_1'=8,'gz'=4] {'gy_1'}, dimensions={0} | all-to-all | bytes 1179648 | tf_op jit(solution)/shard_map/all_to_all | solution.py:26
  45.9 0.0 copy-done.2
  45.9 3.5 %all-to-all-start = ((bf16[8,96,256]{2,1,0:T(8,128)(2,1)}), bf16[8,96,256]{2,1,0:T(8,128)(2,1)S(1)}, u32[]{:S(2)}, u32[]{:S(2)}) async-start(bf16[8,96,256]{2,1,0:T(8,128)(2,1)} %copy-done.2), calls=%async_computation | async-start | bytes 786432 | tf_op jit(solution)/shard_map/all_to_all | solution.py:26
  49.3 3.4 %collective-permute-start = (bf16[8,96,384]{2,1,0:T(8,128)(2,1)S(1)}, bf16[8,96,384]{2,1,0:T(8,128)(2,1)}, u32[]{:S(2)}, u32[]{:S(2)}) collective-permute-start(bf16[8,96,384]{2,1,0:T(8,128)(2,1)S(1)} %all_to_all.26.near), channel_id=1, source_target_pairs={{0,32},{32,0},{1,33},{33,1},{2,34},{34,2},{3,35},{35,3},{4,36},{36... | collective-permute-start | bytes 1769480 | tf_op jit(solution)/shard_map/ppermute | solution.py:287
  52.7 8.4 %all-to-all-done.cols = bf16[8,96,256]{2,1,0:T(8,128)(2,1)S(1)} async-done(((bf16[8,96,256]{2,1,0:T(8,128)(2,1)}), bf16[8,96,256]{2,1,0:T(8,128)(2,1)S(1)}, u32[]{:S(2)}, u32[]{:S(2)}) %all-to-all-start) | async-done | bytes 393248 | tf_op jit(solution)/shard_map/all_to_all | solution.py:26
  61.1 0.0 copy-start.1
  61.1 1.7 %collective-permute-done.far = bf16[8,96,384]{2,1,0:T(8,128)(2,1)} collective-permute-done((bf16[8,96,384]{2,1,0:T(8,128)(2,1)S(1)}, bf16[8,96,384]{2,1,0:T(8,128)(2,1)}, u32[]{:S(2)}, u32[]{:S(2)}) %collective-permute-start) | collective-permute-done | bytes 589856 | tf_op jit(solution)/shard_map/ppermute | solution.py:287
  62.8 2.5 %partial_totals.1 = bf16[32,24,128]{2,1,0:T(8,128)(2,1)S(1)} custom-call(s32[3]{0:T(128)S(1)} %pad_add_fusion._.place, f32[8,128]{1,0:T(8,128)S(1)} %after.1._, bf16[8,96,384]{2,1,0:T(8,128)(2,1)S(1)} %all_to_all.26.near, bf16[8,96,384]{2,1,0:T(8,128)(2,1)} %collective-permute-done.far, bf16[8,96,256]{2,1,0:T(8,128)(2,1)S(1)} %all-to-all-done.cols, ...), custom_call_target="tpu_custom_call" | custom-call | tf_op jit(solution)/shard_map/partial_totals/pallas_call | solution.py:298
  65.3 21.3 %all_to_all.27.arrived = bf16[32,24,128]{2,1,0:T(8,128)(2,1)S(1)} all-to-all(bf16[32,24,128]{2,1,0:T(8,128)(2,1)S(1)} %partial_totals.1), channel_id=1, replica_groups=mesh['gx'=8,'gy_0'=2,'gy_1'=8,'gz'=4] {'gx','gz'}, dimensions={0} | all-to-all | bytes 393216 | tf_op jit(solution)/shard_map/all_to_all | solution.py:26
  86.6 0.0 copy-done.1
  86.6 1.4 %final_shares.1 = bf16[128,4,384]{2,1,0:T(4,128)(2,1)S(1)} custom-call(s32[3]{0:T(128)S(1)} %pad_add_fusion._.place, bf16[32,24,128]{2,1,0:T(8,128)(2,1)S(1)} %all_to_all.27.arrived, bf16[96,384]{1,0:T(8,128)(2,1)S(1)} %get-tuple-element.7.block, bf16[96,4000]{1,0:T(8,128)(2,1)S(1)} %copy-done.1), custom_call_target="tpu_custom_call" | custom-call | tf_op jit(solution)/shard_map/final_shares/pallas_call | solution.py:309
  88.0 25.5 %all_to_all.28.arrived = bf16[128,4,384]{2,1,0:T(4,128)(2,1)S(1)} all-to-all(bf16[128,4,384]{2,1,0:T(4,128)(2,1)S(1)} %final_shares.1), channel_id=1, replica_groups=mesh['gx'=8,'gy_0'=2,'gy_1'=8,'gz'=4] {'gx','gy_0','gy_1'}, dimensions={0} | all-to-all | bytes 786432 | tf_op jit(solution)/shard_map/all_to_all | solution.py:26
  113.5 0.8 outputs.1
  (1 shorter events, 0.0 us)
Async XLA Ops:
  0.6 21.0 %copy-start = (bf16[1536,1,768]{2,0,1:T(8,128)(2,1)S(1)}, bf16[1536,1,768]{2,0,1:T(8,128)(2,1)}, u32[]{:S(2)}) copy-start(bf16[1536,1,768]{2,0,1:T(8,128)(2,1)} %param.5) | copy-start | bytes 7077892
  3.8 42.1 %copy-start.2 = (bf16[8,96,256]{2,1,0:T(8,128)(2,1)}, bf16[8,96,256]{2,1,0:T(8,128)(2,1)S(1)}, u32[]{:S(2)}) copy-start(bf16[8,96,256]{2,1,0:T(8,128)(2,1)S(1)} %get-tuple-element.5) | copy-start | bytes 1179652
  45.9 15.3 %all-to-all-start = ((bf16[8,96,256]{2,1,0:T(8,128)(2,1)}), bf16[8,96,256]{2,1,0:T(8,128)(2,1)S(1)}, u32[]{:S(2)}, u32[]{:S(2)}) async-start(bf16[8,96,256]{2,1,0:T(8,128)(2,1)} %copy-done.2), calls=%async_computation | async-start | bytes 786432 | tf_op jit(solution)/shard_map/all_to_all | solution.py:26
  49.3 13.5 %collective-permute-start = (bf16[8,96,384]{2,1,0:T(8,128)(2,1)S(1)}, bf16[8,96,384]{2,1,0:T(8,128)(2,1)}, u32[]{:S(2)}, u32[]{:S(2)}) collective-permute-start(bf16[8,96,384]{2,1,0:T(8,128)(2,1)S(1)} %all_to_all.26.near), channel_id=1, source_target_pairs={{0,32},{32,0},{1,33},{33,1},{2,34},{34,2},{3,35},{35,3},{4,36},{36... | collective-permute-start | bytes 1769480 | tf_op jit(solution)/shard_map/ppermute | solution.py:287
  61.1 25.5 %copy-start.1 = (bf16[96,4000]{1,0:T(8,128)(2,1)S(1)}, bf16[96,4000]{1,0:T(8,128)(2,1)}, u32[]{:S(2)}) copy-start(bf16[96,4000]{1,0:T(8,128)(2,1)} %colloc.1) | copy-start | bytes 2304004
